TPU v7x, 32 devices: a 4x2x2 block of a 4x4x8 slice. The times are simulated.
32 devices in a mesh: req: 4 (over y, z), cp: 8 (over x, core).
Axes of the slice: x: 4, y: 2, z: 2, core: 2. Of those that a mesh axis runs over, the one named last changes fastest.
The devices are a block of a 4x4x8 slice.
Arguments:
- x: bfloat16 [16384, 2048], P(('req', 'cp')), parts along dimension 0
- pos: int32 [16384], P(('req', 'cp')), parts along dimension 0
- g1: bfloat16 [2, 2048], replicated
- g2: bfloat16 [2, 2048], replicated
- wq: bfloat16 [2, 2048, 2048], replicated
- wk: bfloat16 [2, 2048, 2048], replicated
- wv: bfloat16 [2, 2048, 2048], replicated
- wo: bfloat16 [2, 2048, 2048], replicated
- w1: bfloat16 [2, 2048, 8192], replicated
- w3: bfloat16 [2, 2048, 8192], replicated
- w2: bfloat16 [2, 8192, 2048], replicated
Outputs:
- output 1: bfloat16 [16384, 2048], P(('req', 'cp')), parts along dimension 0
- output 2: bfloat16 [2, 16384, 16, 128], P(None, 'req', 'cp'), parts along dimension 1
- output 3: bfloat16 [2, 16384, 16, 128], P(None, 'req', 'cp'), parts along dimension 1
There are 4 independent parts. A program takes and returns all parts, laid end to end along the dimension named above; an argument that names none is the same for every part.
All inputs are finite; a program needn't handle non-finite values.
Results may differ from a plain program's by a relative error of at most 0.018145.
Values are sent between devices in bfloat16 or wider.
A program may use at most 768 MiB of HBM per device.

v0:
```python
import jax
import jax.numpy as jnp
from jax import lax
from jax.sharding import PartitionSpec as P

HEAD = 128
F32 = jnp.float32
BF16 = jnp.bfloat16


def _norm(x, g):
    x32 = x.astype(F32)
    r = lax.rsqrt(jnp.mean(x32 * x32, axis=-1, keepdims=True) + 1e-5)
    return (x32 * r * g.astype(F32)).astype(BF16)


def _angles(pos):
    half = HEAD // 2
    inv = 1.0 / (10000.0 ** (jnp.arange(half, dtype=F32) * (2.0 / HEAD)))
    ang = pos.astype(F32)[..., None] * inv
    return jnp.cos(ang)[..., None, :], jnp.sin(ang)[..., None, :]


def _rope(t, c, sn):
    half = HEAD // 2
    t1, t2 = t[..., :half], t[..., half:]
    return jnp.concatenate([t1 * c - t2 * sn, t2 * c + t1 * sn], axis=-1)


def _attention(q, kg, vg, mask):
    def one(a):
        qh, kh, vh = a
        sc = jnp.einsum('qd,kd->qk', qh, kh, preferred_element_type=F32) * HEAD ** -0.5
        p = jax.nn.softmax(jnp.where(mask, sc, -jnp.inf), axis=-1).astype(BF16)
        return jnp.dot(p, vh, preferred_element_type=F32).astype(BF16)

    o = lax.map(one, (q.transpose(1, 0, 2), kg.transpose(1, 0, 2), vg.transpose(1, 0, 2)))
    return o.transpose(1, 0, 2).reshape(q.shape[0], -1)


def _natural(a, ncp):
    n, seq = a.shape[0], a.shape[1]
    a = a.reshape((n, ncp, 2, seq // (2 * ncp)) + a.shape[2:])
    a = jnp.concatenate([a[:, :, 0], a[:, ::-1, 1]], axis=1)
    return a.reshape((n, seq) + a.shape[3:])


def solution(mesh):
    ncp = mesh.shape['cp']
    act = P(('req', 'cp'), None)
    cache = P(None, 'req', 'cp', None)

    def body(x, pos, g1, g2, wq, wk, wv, wo, w1, w3, w2):
        s_dev = x.shape[0]
        nh = wq.shape[2] // HEAD
        pos_all = lax.all_gather(pos, 'cp', tiled=True)
        mask = pos_all[None, :] <= pos[:, None]
        c, sn = _angles(pos)
        kl, vl = [], []
        for l in range(wq.shape[0]):
            h = _norm(x, g1[l])
            q = _rope(jnp.dot(h, wq[l], preferred_element_type=F32).reshape(s_dev, nh, HEAD), c, sn).astype(BF16)
            k = _rope(jnp.dot(h, wk[l], preferred_element_type=F32).reshape(s_dev, nh, HEAD), c, sn).astype(BF16)
            v = jnp.dot(h, wv[l], preferred_element_type=F32).astype(BF16).reshape(s_dev, nh, HEAD)
            kg = lax.all_gather(k, 'cp', tiled=True)
            vg = lax.all_gather(v, 'cp', tiled=True)
            o = _attention(q, kg, vg, mask)
            x = (x.astype(F32) + jnp.dot(o, wo[l], preferred_element_type=F32)).astype(BF16)
            h2 = _norm(x, g2[l])
            u = (jax.nn.silu(jnp.dot(h2, w1[l], preferred_element_type=F32))
                 * jnp.dot(h2, w3[l], preferred_element_type=F32)).astype(BF16)
            x = (x.astype(F32) + jnp.dot(u, w2[l], preferred_element_type=F32)).astype(BF16)
            kl.append(k)
            vl.append(v)
        kc = _natural(lax.all_to_all(jnp.stack(kl), 'cp', 2, 1, tiled=True), ncp)
        vc = _natural(lax.all_to_all(jnp.stack(vl), 'cp', 2, 1, tiled=True), ncp)
        return x, kc, vc

    return jax.shard_map(body, mesh=mesh, in_specs=(act, P(('req', 'cp'))) + (P(),) * 9,
                         out_specs=(act, cache, cache), check_vma=False)
```

profile of v0, /device:TPU:81, one launch (start us, length us, event | category | flops | bytes accessed | tf_op | source)
XLA Modules:
  0.0 949.0 jit_solution(387449784183197766)
XLA Ops:
  10.7 11.9 %slice_bitcast_fusion = (bf16[2048,2048]{0,1:T(8,128)(2,1)}, bf16[2048,2048]{0,1:T(8,128)(2,1)}) fusion(bf16[2,2048,2048]{2,1,0:T(8,128)(2,1)} %param.20), kind=kLoop, calls=%fused_computation.64 | loop fusion | bytes 33554432 | tf_op jit(solution)/shard_map/dot_general | solution.py:63
  22.7 12.3 %copy.61 = bf16[2048,2048]{1,0:T(8,128)(2,1)} copy(bf16[2048,2048]{0,1:T(8,128)(2,1)} %get-tuple-element.200) | data formatting | bytes 16777216 | tf_op jit(solution)/shard_map/dot_general | solution.py:63
  35.0 11.8 %slice_bitcast_fusion.1 = (bf16[2048,2048]{0,1:T(8,128)(2,1)}, bf16[2048,2048]{0,1:T(8,128)(2,1)}) fusion(bf16[2,2048,2048]{2,1,0:T(8,128)(2,1)} %param.19), kind=kLoop, calls=%fused_computation.65 | loop fusion | bytes 33554432 | tf_op jit(solution)/shard_map/dot_general | solution.py:62
  46.8 12.5 %copy.60 = bf16[2048,2048]{1,0:T(8,128)(2,1)} copy(bf16[2048,2048]{0,1:T(8,128)(2,1)} %get-tuple-element.202) | data formatting | bytes 16777216 | tf_op jit(solution)/shard_map/dot_general | solution.py:62
  59.3 7.2 fusion.106
  66.6 4.8 fusion.108
  76.4 9.9 %all-gather.8.cloned.1.call-start = ((), (), s32[]{:S(2)}) async-start(), calls=%async_computation.3 | async-start | bytes 18874368 | tf_op jit(solution)/shard_map/all_gather | solution.py:66
  86.3 8.6 fusion.96
  98.2 14.9 %all-gather = s32[8,1,512]{2,1,0:T(1,128)S(1)} all-gather(s32[1,1,512]{2,1,0:T(1,128)S(1)} %bitcast.245), channel_id=1, replica_groups=mesh['req'=4,'cp'=8] {'cp'}, dimensions={0}, use_global_device_ids=true | all-gather | bytes 18432 | tf_op jit(solution)/shard_map/all_gather | solution.py:56
  115.2 48.3 %all-gather.6.cloned.1.call-done = bf16[4096,16,128]{0,2,1:T(8,128)(2,1)} async-done(((bf16[512,16,128]{0,2,1:T(8,128)(2,1)}), bf16[4096,16,128]{0,2,1:T(8,128)(2,1)}) %all-gather.6.cloned.1.call-update) | async-done | bytes 16777232 | tf_op jit(solution)/shard_map/all_gather | solution.py:65
  163.5 84.8 %all-gather.8.cloned.1.call-done = bf16[4096,16,128]{2,0,1:T(8,128)(2,1)} async-done(((bf16[512,16,128]{2,0,1:T(8,128)(2,1)}), bf16[4096,16,128]{2,0,1:T(8,128)(2,1)}) %all-gather.8.cloned.1.call-update) | async-done | bytes 16777232 | tf_op jit(solution)/shard_map/all_gather | solution.py:66
  249.8 123.5 %while.22 = (s32[]{:T(128)}, bf16[16,512,128]{1,2,0:T(8,128)(2,1)}, bf16[16,512,128]{1,2,0:T(8,128)(2,1)}, bf16[16,4096,128]{1,2,0:T(8,128)(2,1)}, bf16[16,4096,...) while((s32[]{:T(128)}, bf16[16,512,128]{1,2,0:T(8,128)(2,1)}, ...), condition=%wide.region_4.5_spmd.clone, body=%wide.region_1.4_spmd.clone.sunk | while | flops 1092680704 | bytes 28080212 | solution.py:37
  249.8 3.0 fusion.176
  257.6 2.9 fusion.176
  265.4 2.9 fusion.176
  273.1 2.9 fusion.176
  280.8 2.9 fusion.176
  288.5 2.9 fusion.176
  296.2 2.9 fusion.176
  303.9 2.9 fusion.176
  311.6 2.9 fusion.176
  319.4 2.9 fusion.176
  327.1 2.9 fusion.176
  334.8 2.9 fusion.176
  342.5 2.9 fusion.176
  350.2 2.9 fusion.176
  357.9 2.9 fusion.176
  365.6 2.9 fusion.176
  373.4 9.0 fusion.72
  383.7 25.7 %fusion.38 = f32[512,8192]{1,0:T(8,128)} fusion(bf16[2,2048,8192]{2,1,0:T(8,128)(2,1)} %param.23, bf16[512,2048]{1,0:T(8,128)(2,1)S(1)} %get-tuple-element.224, f32[2048]{0:T(1024)S(1)} %bitcast.251, f32[512]{0:T(512)S(1)} %add_rsqrt_fusion.2), kind=kOutput, calls=%fused_computation.44 | convolution fusion | flops 17184063488 | bytes 52439040 | tf_op jit(solution)/shard_map/dot_general | solution.py:70
  409.4 27.2 %multiply_convert_fusion.1.clone.3.clone.5 = bf16[512,8192]{1,0:T(8,128)(2,1)} fusion(f32[512,8192]{1,0:T(8,128)} %fusion.38, bf16[2,2048,8192]{2,1,0:T(8,128)(2,1)} %param.24, bf16[512,2048]{1,0:T(8,128)(2,1)} %copy-done.27, f32[2048]{0:T(1024)S(1)} %bitcast.252, f32[512]{0:T(512)S(1)} %add_rsqrt_fusion.2), kind=kOutput, calls=%fused_computation.53.clone.clone.clone.clone.clone.clone.clone.2 | convolution fusion | flops 17209229312 | bytes 60827648 | tf_op jit(solution)/shard_map/dot_general | solution.py:71
  436.5 24.3 %fusion.76 = (f32[512]{0:T(512)S(1)}, bf16[512,2048]{1,0:T(8,128)(2,1)S(1)}) fusion(bf16[2,8192,2048]{2,1,0:T(8,128)(2,1)} %param.25, bf16[512,2048]{1,0:T(8,128)(2,1)} %copy-done.27, bf16[512,8192]{1,0:T(8,128)(2,1)} %multiply_convert_fusion.1.clone.3.clone.5), kind=kOutput, calls=%fused_computation.92 | convolution fusion | flops 17186160640 | bytes 46139392 | tf_op jit(solution)/shard_map/dot_general | solution.py:72
  460.9 9.2 fusion.99
  473.4 12.3 %copy.66 = bf16[2048,2048]{1,0:T(8,128)(2,1)} copy(bf16[2048,2048]{0,1:T(8,128)(2,1)} %get-tuple-element.201) | data formatting | bytes 16777216 | tf_op jit(solution)/shard_map/dot_general | solution.py:62
  485.7 12.3 %copy.67 = bf16[2048,2048]{1,0:T(8,128)(2,1)} copy(bf16[2048,2048]{0,1:T(8,128)(2,1)} %get-tuple-element.199) | data formatting | bytes 16777216 | tf_op jit(solution)/shard_map/dot_general | solution.py:63
  498.0 7.5 fusion.104
  505.6 4.7 fusion.102
  520.9 4.8 all-to-all-start.1
  529.6 69.2 %all-to-all-done.1 = bf16[2,512,16,128]{3,1,0,2:T(8,128)(2,1)} async-done(((bf16[2,512,16,128]{3,1,0,2:T(8,128)(2,1)}), bf16[2,512,16,128]{3,1,0,2:T(8,128)(2,1)}, u32[]{:S(2)}, u32[]{:S(2)}) %all-to-all-start.1) | async-done | bytes 4194336 | tf_op jit(solution)/shard_map/all_to_all | solution.py:76
  598.9 5.5 all-to-all-start
  611.2 35.4 %copy.80 = bf16[2,4096,2,128]{3,2,1,0:T(2,128)(2,1)} copy(bf16[2,4096,2,128]{3,1,2,0:T(8,128)(2,1)S(1)} %bitcast.226) | data formatting | bytes 8388608
  646.6 44.7 %all-to-all-done = bf16[2,512,16,128]{1,3,0,2:T(8,128)(2,1)} async-done(((bf16[2,512,16,128]{1,3,0,2:T(8,128)(2,1)}), bf16[2,512,16,128]{1,3,0,2:T(8,128)(2,1)}, u32[]{:S(2)}, u32[]{:S(2)}) %all-to-all-start) | async-done | bytes 4194336 | tf_op jit(solution)/shard_map/all_to_all | solution.py:75
  691.3 6.9 reshape.195
  698.2 9.9 %fusion.132 = (bf16[2,8,1,256,2,128]{3,2,5,0,4,1:T(2,128)(2,1)}, bf16[2,8,1,256,2,128]{3,2,5,0,4,1:T(2,128)(2,1)}) fusion(bf16[2,8,2,256,2,128]{3,2,5,0,4,1:T(2,128)(2,1)} %reshape.195), kind=kLoop, calls=%fused_computation.150 | loop fusion | bytes 8388608 | tf_op jit(solution)/shard_map/slice | solution.py:44
  708.1 9.4 copy.91
  717.5 11.2 %copy.90 = bf16[2,8,1,256,2,128]{5,4,3,1,0,2:T(2,128)(2,1)} copy(bf16[2,8,1,256,2,128]{3,2,5,0,4,1:T(2,128)(2,1)} %get-tuple-element.211) | data formatting | bytes 4194304
  728.7 2.9 reverse_bitcast_fusion.1
  731.7 9.7 %pad_maximum_fusion = bf16[2,16,256,2,128]{4,3,2,1,0:T(2,128)(2,1)} fusion(bf16[2,8,256,2,128]{4,3,2,1,0:T(2,128)(2,1)} %reverse_bitcast_fusion.1, bf16[2,8,256,2,128]{4,3,2,1,0:T(2,128)(2,1)} %bitcast.238), kind=kLoop, calls=%fused_computation.101 | loop fusion | flops 2097152 | bytes 8388608 | tf_op jit(solution)/shard_map/concatenate | solution.py:44
  741.6 113.3 %while.23 = (s32[]{:T(128)}, bf16[16,512,128]{1,2,0:T(8,128)(2,1)S(1)}, bf16[16,512,128]{1,2,0:T(8,128)(2,1)}, bf16[16,4096,128]{1,2,0:T(8,128)(2,1)}, bf16[16,4...) while((s32[]{:T(128)}, bf16[16,512,128]{1,2,0:T(8,128)(2,1)S(1)}, ...), condition=%wide.region_10.11_spmd.clone, body=%wide.region_7.10_spmd.clone.sunk | while | flops 1092680704 | bytes 28079704 | solution.py:37
  741.6 2.9 fusion.180
  748.6 2.9 fusion.180
  755.7 2.9 fusion.180
  769.9 2.9 fusion.180
  784.0 2.9 fusion.180
  791.1 2.9 fusion.180
  805.3 2.9 fusion.180
  812.4 2.9 fusion.180
  819.4 2.9 fusion.180
  833.6 2.9 fusion.180
  840.7 2.9 fusion.180
  854.8 8.9 fusion.80
  865.1 25.2 %fusion.32 = f32[512,8192]{1,0:T(8,128)} fusion(bf16[2,2048,8192]{2,1,0:T(8,128)(2,1)} %param.23, bf16[512,2048]{1,0:T(8,128)(2,1)S(1)} %get-tuple-element.228, f32[2048]{0:T(1024)S(1)} %bitcast.246, f32[512]{0:T(512)S(1)} %add_rsqrt_fusion), kind=kOutput, calls=%fused_computation.38 | convolution fusion | flops 17184063488 | bytes 52439040 | tf_op jit(solution)/shard_map/dot_general | solution.py:70
  890.4 27.3 %multiply_convert_fusion.clone.7 = bf16[512,8192]{1,0:T(8,128)(2,1)} fusion(f32[512,8192]{1,0:T(8,128)} %fusion.32, bf16[2,2048,8192]{2,1,0:T(8,128)(2,1)} %param.24, bf16[512,2048]{1,0:T(8,128)(2,1)} %copy-done.28, f32[2048]{0:T(1024)S(1)} %bitcast.247, f32[512]{0:T(512)S(1)} %add_rsqrt_fusion), kind=kOutput, calls=%fused_computation.52.clone.clone.clone.clone.clone.2 | convolution fusion | flops 17209229312 | bytes 60827648 | tf_op jit(solution)/shard_map/dot_general | solution.py:71
  917.7 24.6 %fusion.83 = bf16[512,2048]{1,0:T(8,128)(2,1)} fusion(bf16[512,2048]{1,0:T(8,128)(2,1)S(1)} %copy-done.29, bf16[2,8192,2048]{2,1,0:T(8,128)(2,1)} %param.25, bf16[512,8192]{1,0:T(8,128)(2,1)} %multiply_convert_fusion.clone.7), kind=kOutput, calls=%fused_computation.99 | convolution fusion | flops 17183014912 | bytes 46137344 | tf_op jit(solution)/shard_map/dot_general | solution.py:72
  (235 shorter events, 201.0 us)
Async XLA Ops:
  7.2 156.3 %all-gather.6.cloned.1.call-start = ((), (), s32[]{:S(2)}) async-start(), calls=%async_computation.2 | async-start | bytes 18874368 | tf_op jit(solution)/shard_map/all_gather | solution.py:65
  46.8 12.5 %copy-start.13 = (bf16[512,2048]{1,0:T(8,128)(2,1)S(1)}, bf16[512,2048]{1,0:T(8,128)(2,1)}, u32[]{:S(2)}) copy-start(bf16[512,2048]{1,0:T(8,128)(2,1)} %param.15) | copy-start | bytes 6291460
  59.3 7.3 copy-start.6
  66.6 4.9 copy-start.22
  72.0 1.5 copy-start.15
  72.0 1.5 copy-start.17
  73.5 1.0 copy-start
  73.5 1.3 copy-start.2
  76.4 171.9 %all-gather.8.cloned.1.call-start = ((), (), s32[]{:S(2)}) async-start(), calls=%async_computation.3 | async-start | bytes 18874368 | tf_op jit(solution)/shard_map/all_gather | solution.py:66
  94.9 1.3 copy-start.7
  98.0 16.5 %copy-start.19 = (bf16[2,2048]{1,0:T(2,128)(2,1)S(1)}, bf16[2,2048]{1,0:T(2,128)(2,1)}, u32[]{:S(2)}) copy-start(bf16[2,2048]{1,0:T(2,128)(2,1)} %param.18) | copy-start | bytes 24580
  98.1 643.2 %all-gather.12.cloned.1.call-start = ((), (), s32[]{:S(2)}) async-start(), calls=%async_computation.5 | async-start | bytes 18874368 | tf_op jit(solution)/shard_map/all_gather | solution.py:66
  249.8 123.6 %copy-start.14 = (bf16[512,2048]{1,0:T(8,128)(2,1)S(1)}, bf16[512,2048]{1,0:T(8,128)(2,1)}, u32[]{:S(2)}) copy-start(bf16[512,2048]{1,0:T(8,128)(2,1)} %param.15) | copy-start | bytes 6291460
  373.3 9.0 copy-start.20
  382.4 1.3 copy-start.27
  436.5 24.3 %copy-start.25 = (f32[1,2048]{1,0:T(1,128)S(1)}, f32[1,2048]{1,0:T(1,128)}, u32[]{:S(2)}) copy-start(f32[1,2048]{1,0:T(1,128)} %get-tuple-element.219) | copy-start | bytes 24580
  460.8 44.7 %copy-start.26 = (bf16[512,2048]{1,0:T(8,128)(2,1)}, bf16[512,2048]{1,0:T(8,128)(2,1)S(1)}, u32[]{:S(2)}) copy-start(bf16[512,2048]{1,0:T(8,128)(2,1)S(1)} %get-tuple-element.226) | copy-start | bytes 6291460
  470.1 1.3 copy-start.9
  473.3 268.0 %all-gather.10.cloned.1.call-start = ((), (), s32[]{:S(2)}) async-start(), calls=%async_computation.4 | async-start | bytes 18874368 | tf_op jit(solution)/shard_map/all_gather | solution.py:65
  498.0 7.5 copy-start.5
  505.5 4.7 copy-start.16
  505.5 4.7 copy-start.18
  513.1 1.0 copy-start.4
  513.1 2.6 copy-start.8
  515.7 1.6 copy-start.10
  520.9 4.8 copy-start.1
  520.9 4.8 copy-start.3
  520.9 78.0 %all-to-all-start.1 = ((bf16[2,512,16,128]{3,1,0,2:T(8,128)(2,1)}), bf16[2,512,16,128]{3,1,0,2:T(8,128)(2,1)}, u32[]{:S(2)}, u32[]{:S(2)}) async-start(bf16[2,512,16,128]{3,1,0,2:T(8,128)(2,1)} %pad_maximum_fusion.1), calls=%async_computation.1 | async-start | bytes 8388608 | tf_op jit(solution)/shard_map/all_to_all | solution.py:76
  529.6 74.7 %copy-start.11 = (bf16[512,16,64]{0,2,1:T(8,128)(2,1)S(1)}, bf16[512,16,64]{0,2,1:T(8,128)(2,1)}, u32[]{:S(2)}) copy-start(bf16[512,16,64]{0,2,1:T(8,128)(2,1)} %get-tuple-element.213) | copy-start | bytes 3145732
  529.6 74.7 %copy-start.12 = (bf16[512,16,64]{0,2,1:T(8,128)(2,1)S(1)}, bf16[512,16,64]{0,2,1:T(8,128)(2,1)}, u32[]{:S(2)}) copy-start(bf16[512,16,64]{0,2,1:T(8,128)(2,1)} %get-tuple-element.214) | copy-start | bytes 3145732
  598.9 92.4 %all-to-all-start = ((bf16[2,512,16,128]{1,3,0,2:T(8,128)(2,1)}), bf16[2,512,16,128]{1,3,0,2:T(8,128)(2,1)}, u32[]{:S(2)}, u32[]{:S(2)}) async-start(bf16[2,512,16,128]{1,3,0,2:T(8,128)(2,1)} %copy.72), calls=%async_computation | async-start | bytes 8388608 | tf_op jit(solution)/shard_map/all_to_all | solution.py:75
  731.7 9.9 %copy-start.21 = (s32[4096]{0:T(1024)S(1)}, s32[4096]{0:T(1024)}, u32[]{:S(2)}) copy-start(s32[4096]{0:T(1024)} %copy-done.20) | copy-start | bytes 49156
  731.7 9.9 %copy-start.23 = (s32[512]{0:T(512)S(1)}, s32[512]{0:T(512)}, u32[]{:S(2)}) copy-start(s32[512]{0:T(512)} %param.16) | copy-start | bytes 6148
  854.8 10.3 %copy-start.24 = (f32[1,2048]{1,0:T(1,128)S(1)}, f32[1,2048]{1,0:T(1,128)}, u32[]{:S(2)}) copy-start(f32[1,2048]{1,0:T(1,128)} %get-tuple-element.217) | copy-start | bytes 24580
  863.8 1.3 copy-start.28
  890.4 27.3 %copy-start.29 = (bf16[512,2048]{1,0:T(8,128)(2,1)S(1)}, bf16[512,2048]{1,0:T(8,128)(2,1)}, u32[]{:S(2)}) copy-start(bf16[512,2048]{1,0:T(8,128)(2,1)} %copy-done.28) | copy-start | bytes 6291460
Sparse Core Ops, SparseCore 0:
  76.5 86.9 all-gather.5
  165.6 82.5 all-gather.7
  473.4 115.8 all-gather.11
  590.8 131.6 all-gather.9
where the time goes:
time: 961 us; the launch traced here: 949 us
  matrix products  395 us (41%)
  waiting for transfers between devices  247 us (26%)
  local copies, waits for them, and re-layouts  187 us (19%)
  other arithmetic  70 us (7%)
  starting transfers between devices  20.3 us (2%)
  blocking collectives  14.9 us (2%)
  between operations  14.5 us (2%)
    dot_general x32, matrix products, one(): jnp.einsum('qd,kd->qk', qh, kh, preferred_element_type=F32) * HEAD ** (-0.5)  92.1 us
    dot_general x32, matrix products, one(): return jnp.dot(p, vh, preferred_element_type=F32).astype(BF16)  88.2 us
    all_gather x2, waiting for transfers between devices, body(): vg = lax.all_gather(v, 'cp', tiled=True)  84.8 us
    all_to_all x1, waiting for transfers between devices, body(): vc = _natural(lax.all_to_all(jnp.stack(vl), 'cp', 2, 1, tiled=True), ncp)  69.2 us
    unnamed x65, local copies, waits for them, and re-layouts  65.3 us
    dot_general x2, matrix products, body(): jnp.dot(h2, w3[l], preferred_element_type=F32)  54.4 us
    dot_general x2, matrix products, body(): jnp.dot(h2, w1[l], preferred_element_type=F32)  50.9 us
    dot_general x2, matrix products, body(): jnp.dot(u, w2[l], preferred_element_type=F32)  48.9 us
  transfers between devices with their start and end apart: 6, of which 4 were waited for; matrix products, arithmetic and copies ran while one was open for 16% of the time, Pallas kernels for 0%

commit v1 on v0

v1 whole, which is shorter than its diff:
```python
import functools
import math

import jax
import jax.numpy as jnp
from jax import lax
from jax.experimental import pallas as pl
from jax.experimental.pallas import tpu as pltpu
from jax.sharding import PartitionSpec as P

HEAD = 128
TILE = 512
NBUF = 8
F32 = jnp.float32
BF16 = jnp.bfloat16
VMEM_LIMIT = 60 * 1024 * 1024


def _tables(pos):
    half = HEAD // 2
    inv = 1.0 / (10000.0 ** (jnp.arange(half, dtype=F32) * (2.0 / HEAD)))
    ang = pos.astype(F32)[:, None] * inv
    c, s = jnp.cos(ang), jnp.sin(ang)
    return jnp.concatenate([c, c], axis=1), jnp.concatenate([-s, s], axis=1)


def _norm_to(dst, x, g):
    x32 = x.astype(F32)
    r = lax.rsqrt(jnp.mean(x32 * x32, axis=-1, keepdims=True) + 1e-5)
    dst[...] = (x32 * r * g.astype(F32)).astype(BF16)


def _dense_kernel(layer, mlp, qkv, *refs):
    refs = list(refs)
    x_ref = refs.pop(0)
    if mlp:
        o_ref, g2_ref, wo, w1, w3, w2 = refs[:6]
        refs = refs[6:]
    if qkv:
        g1_ref, cos_ref, sin_ref, wq, wk, wv = refs[:6]
        refs = refs[6:]
    if mlp:
        y_ref = refs.pop(0)
    if qkv:
        qkv_ref = refs.pop(0)
    h_s, wbuf, sems = refs[:3]
    if mlp:
        xm_s, u_s = refs[3:5]
    rows, d = x_ref.shape
    nk = wbuf.shape[1]

    segs = []
    base = 0
    if mlp:
        no, nf = wo.shape[2] // TILE, w1.shape[2] // TILE
        kk = w2.shape[1] // nk
        ny = w2.shape[2] // TILE
        b_o, b_1, b_2 = 0, no, no + 2 * nf
        segs.append((b_o, no, lambda i: [(None, wo.at[layer, :, pl.ds(i * TILE, TILE)])]))
        segs.append((b_1, 2 * nf, lambda i: [(0, w1.at[layer, :, pl.ds((i // 2) * TILE, TILE)]),
                                             (1, w3.at[layer, :, pl.ds((i // 2) * TILE, TILE)])]))
        segs.append((b_2, ny * kk, lambda i: [(None, w2.at[layer, pl.ds((i % kk) * nk, nk),
                                                          pl.ds((i // kk) * TILE, TILE)])]))
        base = b_2 + ny * kk
    if qkv:
        lq = layer + 1
        nq = wq.shape[2] // TILE
        b_q = base
        segs.append((b_q, 3 * nq, lambda i: [(0, wq.at[lq, :, pl.ds((i // 3) * TILE, TILE)]),
                                             (1, wk.at[lq, :, pl.ds((i // 3) * TILE, TILE)]),
                                             (2, wv.at[lq, :, pl.ds((i // 3) * TILE, TILE)])]))
        base = b_q + 3 * nq
    total = base

    def start(t):
        slot = lax.rem(t, NBUF) if not isinstance(t, int) else t % NBUF
        for b, n, srcs in segs:
            if isinstance(t, int):
                if b <= t < b + n:
                    lst = srcs(t - b)
                    src = lst[(t - b) % len(lst)][1]
                    pltpu.make_async_copy(src, wbuf.at[slot], sems.at[slot]).start()
                continue
            i = t - b
            lst = srcs(i)
            for which, src in lst:
                cond = (t >= b) & (t < b + n)
                if which is not None:
                    cond = cond & (lax.rem(i, len(lst)) == which)

                @pl.when(cond)
                def _(src=src):
                    pltpu.make_async_copy(src, wbuf.at[slot], sems.at[slot]).start()

    any_src = segs[0][2](0)[0][1]

    def ready(t):
        slot = lax.rem(t, NBUF)
        pltpu.make_async_copy(any_src, wbuf.at[slot], sems.at[slot]).wait()
        return slot

    for t in range(min(NBUF, total)):
        start(t)

    if mlp:
        for j in range(o_ref.shape[0]):
            w = o_ref.shape[2]
            h_s[:, j * w:(j + 1) * w] = o_ref[j]

        @pl.loop(0, no)
        def _(i):
            t = b_o + i
            slot = ready(t)
            col = pl.ds(pl.multiple_of(i * TILE, TILE), TILE)
            r = jnp.dot(h_s[...], wbuf[slot], preferred_element_type=F32)
            xm_s[:, col] = (x_ref[:, col].astype(F32) + r).astype(BF16)
            start(t + NBUF)

        _norm_to(h_s, xm_s[...], g2_ref[...])

        @pl.loop(0, nf)
        def _(i):
            t = b_1 + 2 * i
            s1 = ready(t)
            s3 = ready(t + 1)
            a = jnp.dot(h_s[...], wbuf[s1], preferred_element_type=F32)
            b = jnp.dot(h_s[...], wbuf[s3], preferred_element_type=F32)
            col = pl.ds(pl.multiple_of(i * TILE, TILE), TILE)
            u_s[:, col] = (a * jax.nn.sigmoid(a) * b).astype(BF16)
            start(t + NBUF)
            start(t + 1 + NBUF)

        @pl.loop(0, ny)
        def _(i):
            t = b_2 + kk * i
            acc = None
            for k in range(kk):
                slot = ready(t + k)
                r = jnp.dot(u_s[:, k * nk:(k + 1) * nk], wbuf[slot], preferred_element_type=F32)
                acc = r if acc is None else acc + r
            col = pl.ds(pl.multiple_of(i * TILE, TILE), TILE)
            y_ref[:, col] = (xm_s[:, col].astype(F32) + acc).astype(BF16)
            for k in range(kk):
                start(t + k + NBUF)

    if qkv:
        _norm_to(h_s, (y_ref if mlp else x_ref)[...], g1_ref[...])
        width = qkv_ref.shape[3]
        per = TILE // width

        @pl.loop(0, nq)
        def _(i):
            t = b_q + 3 * i
            for m in range(3):
                slot = ready(t + m)
                r = jnp.dot(h_s[...], wbuf[slot], preferred_element_type=F32)
                for a in range(TILE // HEAD):
                    z = r[:, a * HEAD:(a + 1) * HEAD]
                    if m < 2:
                        z = z * cos_ref[...] + pltpu.roll(z, HEAD // 2, 1) * sin_ref[...]
                    lane = (a * HEAD) % width
                    qkv_ref[i * per + (a * HEAD) // width, m, :, lane:lane + HEAD] = z.astype(BF16)
            for m in range(3):
                start(t + m + NBUF)


def _dense(layer, x, o, tabs, w, ncp, mlp, qkv):
    g1, g2, wq, wk, wv, wo, w1, w3, w2 = w
    rows, d = x.shape
    ff = w1.shape[2]
    width = wq.shape[2] // ncp
    anyspace = pl.BlockSpec(memory_space=pl.ANY)
    vmem = pl.BlockSpec(memory_space=pltpu.VMEM)
    ins, specs = [x], [vmem]
    outs, ospecs = [], []
    scratch = [pltpu.VMEM((rows, d), BF16), pltpu.VMEM((NBUF, d, TILE), BF16), pltpu.SemaphoreType.DMA((NBUF,))]
    flops = 0
    if mlp:
        ins += [o, g2[layer:layer + 1], wo, w1, w3, w2]
        specs += [vmem, vmem] + [anyspace] * 4
        outs.append(jax.ShapeDtypeStruct((rows, d), BF16))
        ospecs.append(vmem)
        scratch += [pltpu.VMEM((rows, d), BF16), pltpu.VMEM((rows, ff), BF16)]
        flops += 2 * rows * d * (d + 3 * ff)
    if qkv:
        ins += [g1[layer + 1:layer + 2], tabs[0], tabs[1], wq, wk, wv]
        specs += [vmem] * 3 + [anyspace] * 3
        outs.append(jax.ShapeDtypeStruct((ncp, 3, rows, width), BF16))
        ospecs.append(vmem)
        flops += 2 * rows * d * 3 * wq.shape[2]
    return pl.pallas_call(
        functools.partial(_dense_kernel, layer, mlp, qkv),
        out_shape=outs,
        in_specs=specs,
        out_specs=ospecs,
        scratch_shapes=scratch,
        compiler_params=pltpu.CompilerParams(vmem_limit_bytes=VMEM_LIMIT),
        cost_estimate=pl.CostEstimate(flops=flops, bytes_accessed=flops // rows, transcendentals=0),
        name=f"dense_{layer + 1}_{int(mlp)}{int(qkv)}",
    )(*ins)


def _attn_kernel(late, first, *refs):
    refs = list(refs)
    qkv_ref = refs.pop(0)
    pre_ref = refs.pop(0) if late else None
    if not first:
        refs = refs[2:]
    o_ref, kc_ref, vc_ref, acc_s, m_s, il_s = refs
    p = pl.program_id(0)
    npair = qkv_ref.shape[0] // 2
    seg, width = qkv_ref.shape[2], qkv_ref.shape[3]
    nh = width // HEAD
    bq = 2 * seg
    scale = HEAD ** -0.5 * math.log2(math.e)

    for which, out in ((1, kc_ref), (2, vc_ref)):
        for i in range(2):
            src = qkv_ref[2 * p + (1 - i if late else i), which]
            for h in range(nh):
                il_s[pl.ds(i * seg * nh + h, seg, stride=nh), :] = src[:, h * HEAD:(h + 1) * HEAD].astype(F32)
        out[0] = il_s[...].astype(BF16)

    ones = jnp.ones((bq, HEAD), BF16)

    def block(ref, j, which, h):
        return ref[pl.ds(2 * j, 2), which, :, h * HEAD:(h + 1) * HEAD].reshape(bq, HEAD)

    def wide(a, n):
        return jnp.concatenate([a] * n, axis=1)

    def scores(ref, j, h):
        return lax.dot_general(block(qkv_ref, p, 0, h), block(ref, j, 1, h), (((1,), (1,)), ((), ())),
                               preferred_element_type=F32)

    r = lax.broadcasted_iota(jnp.int32, (bq, bq), 0)
    c = lax.broadcasted_iota(jnp.int32, (bq, bq), 1)
    if late:
        r = jnp.where(r < seg, r + seg, r - seg)
        c = jnp.where(c < seg, c + seg, c - seg)
    mask = c <= r
    for h in range(nh):
        s = jnp.where(mask, scores(qkv_ref, p, h), -jnp.inf)
        m = jnp.broadcast_to(jnp.max(s, axis=1, keepdims=True), (bq, HEAD))
        pr = jnp.exp2((s - wide(m, bq // HEAD)) * scale).astype(BF16)
        v = jnp.concatenate([block(qkv_ref, p, 2, h), ones], axis=1)
        acc_s[h] = jnp.dot(pr, v, preferred_element_type=F32)
        m_s[h] = m

    def full(ref, j):
        for h in range(nh):
            s = scores(ref, j, h)
            old = m_s[h]
            m = jnp.maximum(old, jnp.broadcast_to(jnp.max(s, axis=1, keepdims=True), (bq, HEAD)))
            pr = jnp.exp2((s - wide(m, bq // HEAD)) * scale).astype(BF16)
            v = jnp.concatenate([block(ref, j, 2, h), ones], axis=1)
            alpha = jnp.exp2((old - m) * scale)
            acc_s[h] = acc_s[h] * wide(alpha, 2) + jnp.dot(pr, v, preferred_element_type=F32)
            m_s[h] = m

    if late:
        @pl.loop(0, npair)
        def _(j):
            full(pre_ref, j)

        @pl.loop(p + 1, npair)
        def _(j):
            full(qkv_ref, j)
    else:
        @pl.loop(0, p)
        def _(j):
            full(qkv_ref, j)

    for h in range(nh):
        o = (acc_s[h, :, :HEAD] / acc_s[h, :, HEAD:]).astype(BF16)
        o_ref[:, :, h * HEAD:(h + 1) * HEAD] = o.reshape(2, seg, HEAD)


def _attention(layer, layers, late, qkv, pre, caches):
    ncp, _, seg, width = qkv.shape
    nh = width // HEAD
    npair = ncp // 2
    rows = 2 * seg * nh
    whole = pl.BlockSpec((ncp, 3, seg, width), lambda p: (0, 0, 0, 0))
    ins, specs = [qkv], [whole]
    if late:
        ins.append(pre)
        specs.append(whole)
    alias = {}
    if caches is not None:
        alias = {len(ins): 1, len(ins) + 1: 2}
        ins += list(caches)
        specs += [pl.BlockSpec(memory_space=pl.ANY)] * 2
    where = (lambda p: (layer, 2 * npair - 1 - p, 0)) if late else (lambda p: (layer, p, 0))
    cache = jax.ShapeDtypeStruct((layers, 2 * ncp * seg * nh, HEAD), BF16)
    pairs = (ncp * seg) ** 2 // 2 * (3 if late else 1) * nh
    o, kc, vc = pl.pallas_call(
        functools.partial(_attn_kernel, late, caches is None),
        grid=(npair,),
        out_shape=[jax.ShapeDtypeStruct((ncp, seg, width), BF16), cache, cache],
        in_specs=specs,
        out_specs=[pl.BlockSpec((2, seg, width), lambda p: (p, 0, 0)),
                   pl.BlockSpec((1, rows, HEAD), where), pl.BlockSpec((1, rows, HEAD), where)],
        scratch_shapes=[pltpu.VMEM((nh, 2 * seg, 2 * HEAD), F32), pltpu.VMEM((nh, 2 * seg, HEAD), F32),
                        pltpu.VMEM((rows, HEAD), F32)],
        input_output_aliases=alias,
        compiler_params=pltpu.CompilerParams(vmem_limit_bytes=VMEM_LIMIT, dimension_semantics=("arbitrary",)),
        cost_estimate=pl.CostEstimate(flops=pairs * HEAD * 8, bytes_accessed=8 * ncp * seg * width * 2,
                                      transcendentals=pairs),
        name=f"attn_{layer}_{int(late)}",
    )(*ins)
    return o, (kc, vc)


def solution(mesh):
    ncp = mesh.shape['cp']
    act = P(('req', 'cp'), None)
    cache = P(None, 'req', 'cp', None)

    def swap(a):
        return lax.all_to_all(a, 'cp', 0, 0, tiled=True)

    def body(x, pos, g1, g2, wq, wk, wv, wo, w1, w3, w2):
        w = (g1, g2, wq, wk, wv, wo, w1, w3, w2)
        layers = wq.shape[0]
        seg = x.shape[0] // 2
        cos, sin = _tables(pos)
        tabs = [(cos[:seg], sin[:seg]), (cos[seg:], sin[seg:])]
        xs = [x[:seg], x[seg:]]
        qkv = [_dense(-1, xs[i], None, tabs[i], w, ncp, False, True)[0] for i in range(2)]
        caches = None
        for l in range(layers):
            more = l + 1 < layers
            ra = swap(qkv[0])
            qb, ra = lax.optimization_barrier((qkv[1], ra))
            rb = swap(qb)
            oa, caches = _attention(l, layers, False, ra, None, caches)
            res = _dense(l, xs[0], swap(oa), tabs[0], w, ncp, True, more)
            ob, caches = _attention(l, layers, True, rb, ra, caches)
            res_b = _dense(l, xs[1], swap(ob), tabs[1], w, ncp, True, more)
            xs = [res[0], res_b[0]]
            if more:
                qkv = [res[1], res_b[1]]
        kc, vc = (a.reshape(layers, -1, wq.shape[2] // ncp // HEAD, HEAD) for a in caches)
        return jnp.concatenate(xs, axis=0), kc, vc

    return jax.shard_map(body, mesh=mesh, in_specs=(act, P(('req', 'cp'))) + (P(),) * 9,
                         out_specs=(act, cache, cache), check_vma=False)
```

time: 961 us -> 419 us (0.44); the launches traced: 949 us -> 418 us
  matrix products: 395 us -> 0 us
  Pallas kernels: 0 us -> 295 us
  local copies, waits for them, and re-layouts: 187 us -> 6.98 us
  waiting for transfers between devices: 247 us -> 69.2 us
  other arithmetic: 70 us -> 5.48 us
  starting transfers between devices: 20.3 us -> 40.2 us
  blocking collectives: 14.9 us -> 0 us
  between operations: 14.5 us -> 0.78 us
    dot_general x78 -> x0, matrix products: 395 us -> none  [the longest x32 92.1 us: one(): jnp.einsum('qd,kd->qk', qh, kh, preferred_element_type=F32) * HEAD ** (-0.5)]
    pallas_call x0 -> x10, Pallas kernels: none -> 295 us  [the longest x6 204 us: _dense(): pl.pallas_call(functools.partial(_dense_kernel, layer, mlp, qkv), out_sha...]
    all_gather x4 -> x0, waiting for transfers between devices: 133 us -> none  [the longest x2 84.8 us: body(): vg = lax.all_gather(v, 'cp', tiled=True)]
    dot_general x6 -> x0, local copies, waits for them, and re-layouts: 73.2 us -> none  [the longest x3 36.6 us: body(): jnp.dot(h, wq[l], preferred_element_type=F32).reshape(s_dev, nh, HEAD)]
    unnamed x65 -> x18, local copies, waits for them, and re-layouts: 65.3 us -> 2.62 us
    all_to_all x2 -> x8, waiting for transfers between devices: 114 us -> 69.2 us  [swap(): return lax.all_to_all(a, 'cp', 0, 0, tiled=True)]
    reduce_sum x33 -> x0, other arithmetic: 43.1 us -> none  [the longest x32 41.1 us: one(): p = jax.nn.softmax(jnp.where(mask, sc, -jnp.inf), axis=-1).astype(BF16)]
    all_to_all x2 -> x8, starting transfers between devices: 10.2 us -> 40.2 us  [swap(): return lax.all_to_all(a, 'cp', 0, 0, tiled=True)]
  transfers between devices with their start and end apart: 6 -> 8, of which waited for: 4 -> 3; matrix products, arithmetic and copies ran while one was open for 16% -> 0% of each run, Pallas kernels for 0% -> 58%
where the time goes in v1:
time: 419 us; the launch traced here: 418 us
  Pallas kernels  295 us (70%)
  waiting for transfers between devices  69.2 us (17%)
  starting transfers between devices  40.2 us (10%)
  local copies, waits for them, and re-layouts  6.98 us (2%)
  other arithmetic  5.48 us (1%)
    pallas_call x6, Pallas kernels, _dense(): pl.pallas_call(functools.partial(_dense_kernel, layer, mlp, qkv), out_sha...  204 us
    pallas_call x4, Pallas kernels, _attention(): pl.pallas_call(functools.partial(_attn_kernel, late, caches is None), gri...  91.3 us
    all_to_all x8, waiting for transfers between devices, swap(): return lax.all_to_all(a, 'cp', 0, 0, tiled=True)  69.2 us
    all_to_all x8, starting transfers between devices, swap(): return lax.all_to_all(a, 'cp', 0, 0, tiled=True)  40.2 us
  transfers between devices with their start and end apart: 8, of which 3 were waited for; matrix products, arithmetic and copies ran while one was open for 0% of the time, Pallas kernels for 58%

profile of v1, /device:TPU:81, one launch (start us, length us, event | category | flops | bytes accessed | tf_op | source)
XLA Modules:
  0.0 417.6 jit_solution(9283088511955041562)
XLA Ops:
  0.6 0.0 copy-start.7
  0.7 0.7 convert_element_type.3
  1.3 3.1 fusion.3
  4.5 0.0 copy-done.7
  4.5 0.6 fusion.5
  5.1 1.0 multiply_sine_fusion
  6.1 1.0 pad_maximum_fusion.1
  7.1 14.2 %dense_0_01.3 = bf16[8,3,256,256]{3,2,1,0:T(8,128)(2,1)} custom-call(bf16[256,2048]{1,0:T(8,128)(2,1)} %get-tuple-element.43.refs_0_, bf16[1,2048]{1,0:T(2,128)(2,1)} %get-tuple-element.52.refs_1_, f32[256,128]{1,0:T(8,128)} %get-tuple-element.57.refs_2_.refs_8_, f32[256,128]{1,0:T(8,128)} %get-tuple-element.45.refs_3_.refs_9_, ...), custom_call_target="tpu_custom_call" | custom-call | flops 6442450944 | bytes 25165824 | tf_op jit(solution)/shard_map/dense_0_01/pallas_call | solution.py:191
  21.3 6.0 %all-to-all-start = ((bf16[8,3,256,256]{3,2,1,0:T(8,128)(2,1)}), bf16[8,3,256,256]{3,2,1,0:T(8,128)(2,1)S(1)}, u32[]{:S(2)}, u32[]{:S(2)}) async-start(bf16[8,3,256,256]{3,2,1,0:T(8,128)(2,1)} %dense_0_01.3), calls=%async_computation | async-start | bytes 6291456 | tf_op jit(solution)/shard_map/all_to_all | solution.py:321
  27.3 14.3 %dense_0_01.2 = bf16[8,3,256,256]{3,2,1,0:T(8,128)(2,1)} custom-call(bf16[256,2048]{1,0:T(8,128)(2,1)} %get-tuple-element.44.refs_0_, bf16[1,2048]{1,0:T(2,128)(2,1)} %get-tuple-element.52.refs_1_, f32[256,128]{1,0:T(8,128)} %get-tuple-element.56.refs_2_.refs_8_, f32[256,128]{1,0:T(8,128)} %get-tuple-element.46.refs_3_.refs_9_, ...), custom_call_target="tpu_custom_call" | custom-call | flops 6442450944 | bytes 25165824 | tf_op jit(solution)/shard_map/dense_0_01/pallas_call | solution.py:191
  41.6 0.0 copy-start.8
  41.6 23.0 %all-to-all-done.refs_0_.refs_1_ = bf16[8,3,256,256]{3,2,1,0:T(8,128)(2,1)S(1)} async-done(((bf16[8,3,256,256]{3,2,1,0:T(8,128)(2,1)}), bf16[8,3,256,256]{3,2,1,0:T(8,128)(2,1)S(1)}, u32[]{:S(2)}, u32[]{:S(2)}) %all-to-all-start) | async-done | bytes 3145760 | tf_op jit(solution)/shard_map/all_to_all | solution.py:321
  64.5 0.0 copy-start.5
  64.6 5.5 %all-to-all-start.2 = ((bf16[8,3,256,256]{3,2,1,0:T(8,128)(2,1)}), bf16[8,3,256,256]{3,2,1,0:T(8,128)(2,1)}, u32[]{:S(2)}, u32[]{:S(2)}) async-start(bf16[8,3,256,256]{3,2,1,0:T(8,128)(2,1)} %dense_0_01.2), calls=%async_computation.2 | async-start | bytes 6291456 | tf_op jit(solution)/shard_map/all_to_all | solution.py:321
  70.1 0.0 copy-done.8
  70.1 0.6 fusion.4
  70.7 0.0 copy-done.5
  70.7 13.9 %attn_0_0.1 = (bf16[8,256,256]{2,1,0:T(8,128)(2,1)}, bf16[2,8192,128]{2,1,0:T(8,128)(2,1)}, bf16[2,8192,128]{2,1,0:T(8,128)(2,1)}) custom-call(bf16[8,3,256,256]{3,2,1,0:T(8,128)(2,1)} %copy-done.5), custom_call_target="tpu_custom_call" | custom-call | flops 4294967296 | bytes 8388608 | tf_op jit(solution)/shard_map/attn_0_0/pallas_call | solution.py:297
  84.6 22.9 %all-to-all-done.2.refs_0_ = bf16[8,3,256,256]{3,2,1,0:T(8,128)(2,1)} async-done(((bf16[8,3,256,256]{3,2,1,0:T(8,128)(2,1)}), bf16[8,3,256,256]{3,2,1,0:T(8,128)(2,1)}, u32[]{:S(2)}, u32[]{:S(2)}) %all-to-all-start.2) | async-done | bytes 3145760 | tf_op jit(solution)/shard_map/all_to_all | solution.py:321
  107.5 4.5 %all-to-all-start.1 = ((bf16[8,256,256]{2,1,0:T(8,128)(2,1)}), bf16[8,256,256]{2,1,0:T(8,128)(2,1)S(1)}, u32[]{:S(2)}, u32[]{:S(2)}) async-start(bf16[8,256,256]{2,1,0:T(8,128)(2,1)} %get-tuple-element.24), calls=%async_computation.1 | async-start | bytes 2097152 | tf_op jit(solution)/shard_map/all_to_all | solution.py:321
  112.1 31.7 %attn_0_1.1 = (bf16[8,256,256]{2,1,0:T(8,128)(2,1)}, bf16[2,8192,128]{2,1,0:T(8,128)(2,1)}, bf16[2,8192,128]{2,1,0:T(8,128)(2,1)}) custom-call(bf16[8,3,256,256]{3,2,1,0:T(8,128)(2,1)} %all-to-all-done.2.refs_0_, bf16[8,3,256,256]{3,2,1,0:T(8,128)(2,1)} %copy-done.5, ...), custom_call_target="tpu_custom_call", output_to_operand_aliasing={{1}: (2, {}), {2}: (3, {})} | custom-call | flops 12884901888 | bytes 8388608 | tf_op jit(solution)/shard_map/attn_0_1/pallas_call | solution.py:297
  143.8 0.0 all-to-all-done.1.refs_1_
  143.8 0.0 copy-start
  143.8 4.9 %all-to-all-start.3 = ((bf16[8,256,256]{2,1,0:T(8,128)(2,1)}), bf16[8,256,256]{2,1,0:T(8,128)(2,1)S(1)}, u32[]{:S(2)}, u32[]{:S(2)}) async-start(bf16[8,256,256]{2,1,0:T(8,128)(2,1)} %get-tuple-element.29), calls=%async_computation.3 | async-start | bytes 2097152 | tf_op jit(solution)/shard_map/all_to_all | solution.py:321
  148.7 0.0 copy-done
  148.7 49.4 %dense_1_11.2 = (bf16[256,2048]{1,0:T(8,128)(2,1)}, bf16[8,3,256,256]{3,2,1,0:T(8,128)(2,1)}) custom-call(bf16[256,2048]{1,0:T(8,128)(2,1)} %get-tuple-element.43.refs_0_, bf16[8,256,256]{2,1,0:T(8,128)(2,1)} %copy-done, bf16[1,2048]{1,0:T(2,128)(2,1)} %get-tuple-element.50.refs_2_, bf16[2,2048,2048]{2,1,0:T(8,128)(2,1)} %refs_3_.7, ...), custom_call_target="tpu_custom_call" | custom-call | flops 34359738368 | bytes 134217728 | tf_op jit(solution)/shard_map/dense_1_11/pallas_call | solution.py:191
  198.1 0.0 all-to-all-done.3.refs_1_
  198.1 0.0 copy-start.1
  198.1 4.8 %all-to-all-start.4 = ((bf16[8,3,256,256]{3,2,1,0:T(8,128)(2,1)}), bf16[8,3,256,256]{3,2,1,0:T(8,128)(2,1)}, u32[]{:S(2)}, u32[]{:S(2)}) async-start(bf16[8,3,256,256]{3,2,1,0:T(8,128)(2,1)} %get-tuple-element.31), calls=%async_computation.4 | async-start | bytes 6291456 | tf_op jit(solution)/shard_map/all_to_all | solution.py:321
  202.9 0.0 copy-done.1
  202.9 49.5 %dense_1_11.3 = (bf16[256,2048]{1,0:T(8,128)(2,1)}, bf16[8,3,256,256]{3,2,1,0:T(8,128)(2,1)}) custom-call(bf16[256,2048]{1,0:T(8,128)(2,1)} %get-tuple-element.44.refs_0_, bf16[8,256,256]{2,1,0:T(8,128)(2,1)} %copy-done.1, bf16[1,2048]{1,0:T(2,128)(2,1)} %get-tuple-element.50.refs_2_, bf16[2,2048,2048]{2,1,0:T(8,128)(2,1)} %refs_3_.7, ...), custom_call_target="tpu_custom_call" | custom-call | flops 34359738368 | bytes 134217728 | tf_op jit(solution)/shard_map/dense_1_11/pallas_call | solution.py:191
  252.4 0.0 all-to-all-done.4.refs_0_.refs_1_
  252.4 4.8 %all-to-all-start.6 = ((bf16[8,3,256,256]{3,2,1,0:T(8,128)(2,1)}), bf16[8,3,256,256]{3,2,1,0:T(8,128)(2,1)S(1)}, u32[]{:S(2)}, u32[]{:S(2)}) async-start(bf16[8,3,256,256]{3,2,1,0:T(8,128)(2,1)} %get-tuple-element.37), calls=%async_computation.6 | async-start | bytes 6291456 | tf_op jit(solution)/shard_map/all_to_all | solution.py:321
  257.2 13.9 %attn_1_0.1 = (bf16[8,256,256]{2,1,0:T(8,128)(2,1)}, bf16[2,8192,128]{2,1,0:T(8,128)(2,1)}, bf16[2,8192,128]{2,1,0:T(8,128)(2,1)}) custom-call(bf16[8,3,256,256]{3,2,1,0:T(8,128)(2,1)} %all-to-all-done.4.refs_0_.refs_1_, bf16[2,8192,128]{2,1,0:T(8,128)(2,1)} %get-tuple-element.33.refs_1_, ...), custom_call_target="tpu_custom_call", output_to_operand_aliasing={{1}: (1, {}), {2}: (2, {})} | custom-call | flops 4294967296 | bytes 8388608 | tf_op jit(solution)/shard_map/attn_1_0/pallas_call | solution.py:297
  271.2 23.3 %all-to-all-done.6.refs_0_ = bf16[8,3,256,256]{3,2,1,0:T(8,128)(2,1)S(1)} async-done(((bf16[8,3,256,256]{3,2,1,0:T(8,128)(2,1)}), bf16[8,3,256,256]{3,2,1,0:T(8,128)(2,1)S(1)}, u32[]{:S(2)}, u32[]{:S(2)}) %all-to-all-start.6) | async-done | bytes 3145760 | tf_op jit(solution)/shard_map/all_to_all | solution.py:321
  294.5 0.0 copy-start.6
  294.5 1.6 copy-done.6
  296.1 4.7 %all-to-all-start.5 = ((bf16[8,256,256]{2,1,0:T(8,128)(2,1)}), bf16[8,256,256]{2,1,0:T(8,128)(2,1)S(1)}, u32[]{:S(2)}, u32[]{:S(2)}) async-start(bf16[8,256,256]{2,1,0:T(8,128)(2,1)} %get-tuple-element.35), calls=%async_computation.5 | async-start | bytes 2097152 | tf_op jit(solution)/shard_map/all_to_all | solution.py:321
  300.8 31.7 %attn_1_1.1 = (bf16[8,256,256]{2,1,0:T(8,128)(2,1)}, bf16[2,8192,128]{2,1,0:T(8,128)(2,1)}, bf16[2,8192,128]{2,1,0:T(8,128)(2,1)}) custom-call(bf16[8,3,256,256]{3,2,1,0:T(8,128)(2,1)} %copy-done.6, bf16[8,3,256,256]{3,2,1,0:T(8,128)(2,1)} %all-to-all-done.4.refs_0_.refs_1_, ...), custom_call_target="tpu_custom_call", output_to_operand_aliasing={{1}: (2, {}), {2}: (3, {})} | custom-call | flops 12884901888 | bytes 8388608 | tf_op jit(solution)/shard_map/attn_1_1/pallas_call | solution.py:297
  332.5 0.0 all-to-all-done.5.refs_1_
  332.5 0.0 copy-start.2
  332.5 4.9 %all-to-all-start.7 = ((bf16[8,256,256]{2,1,0:T(8,128)(2,1)}), bf16[8,256,256]{2,1,0:T(8,128)(2,1)S(1)}, u32[]{:S(2)}, u32[]{:S(2)}) async-start(bf16[8,256,256]{2,1,0:T(8,128)(2,1)} %get-tuple-element.40), calls=%async_computation.7 | async-start | bytes 2097152 | tf_op jit(solution)/shard_map/all_to_all | solution.py:321
  337.4 0.0 copy-done.2
  337.4 38.2 %dense_2_10.2 = bf16[256,2048]{1,0:T(8,128)(2,1)} custom-call(bf16[256,2048]{1,0:T(8,128)(2,1)} %get-tuple-element.25.refs_0_, bf16[8,256,256]{2,1,0:T(8,128)(2,1)} %copy-done.2, bf16[1,2048]{1,0:T(2,128)(2,1)} %get-tuple-element.49.refs_2_, bf16[2,2048,2048]{2,1,0:T(8,128)(2,1)} %refs_3_.7, bf16[2,2048,8192]{2,1,0:T(8,128)(2,1)} %refs_4_.11, ...), custom_call_target="tpu_custom_call" | custom-call | flops 27917287424 | bytes 109051904 | tf_op jit(solution)/shard_map/dense_2_10/pallas_call | solution.py:191
  375.6 0.0 all-to-all-done.7.refs_1_
  375.6 0.0 copy-start.3
  375.6 1.0 copy-done.3
  376.5 0.0 copy-start.4
  376.5 38.2 %dense_2_10.3 = bf16[256,2048]{1,0:T(8,128)(2,1)} custom-call(bf16[256,2048]{1,0:T(8,128)(2,1)} %get-tuple-element.36.refs_0_, bf16[8,256,256]{2,1,0:T(8,128)(2,1)} %copy-done.3, bf16[1,2048]{1,0:T(2,128)(2,1)} %get-tuple-element.49.refs_2_, bf16[2,2048,2048]{2,1,0:T(8,128)(2,1)} %refs_3_.7, bf16[2,2048,8192]{2,1,0:T(8,128)(2,1)} %refs_4_.11, ...), custom_call_target="tpu_custom_call" | custom-call | flops 27917287424 | bytes 109051904 | tf_op jit(solution)/shard_map/dense_2_10/pallas_call | solution.py:191
  414.8 0.0 copy-done.4
  414.8 2.8 pad_maximum_fusion
  (1 shorter events, 0.0 us)
Async XLA Ops:
  0.6 3.8 copy-start.7
  21.3 43.3 %all-to-all-start = ((bf16[8,3,256,256]{3,2,1,0:T(8,128)(2,1)}), bf16[8,3,256,256]{3,2,1,0:T(8,128)(2,1)S(1)}, u32[]{:S(2)}, u32[]{:S(2)}) async-start(bf16[8,3,256,256]{3,2,1,0:T(8,128)(2,1)} %dense_0_01.3), calls=%async_computation | async-start | bytes 6291456 | tf_op jit(solution)/shard_map/all_to_all | solution.py:321
  41.6 28.5 %copy-start.8 = (bf16[2,2048]{1,0:T(2,128)(2,1)S(1)}, bf16[2,2048]{1,0:T(2,128)(2,1)}, u32[]{:S(2)}) copy-start(bf16[2,2048]{1,0:T(2,128)(2,1)} %param.14) | copy-start | bytes 24580
  64.5 6.1 %copy-start.5 = (bf16[8,3,256,256]{3,2,1,0:T(8,128)(2,1)}, bf16[8,3,256,256]{3,2,1,0:T(8,128)(2,1)S(1)}, u32[]{:S(2)}) copy-start(bf16[8,3,256,256]{3,2,1,0:T(8,128)(2,1)S(1)} %all-to-all-done.refs_0_.refs_1_) | copy-start | bytes 9437188
  64.6 43.0 %all-to-all-start.2 = ((bf16[8,3,256,256]{3,2,1,0:T(8,128)(2,1)}), bf16[8,3,256,256]{3,2,1,0:T(8,128)(2,1)}, u32[]{:S(2)}, u32[]{:S(2)}) async-start(bf16[8,3,256,256]{3,2,1,0:T(8,128)(2,1)} %dense_0_01.2), calls=%async_computation.2 | async-start | bytes 6291456 | tf_op jit(solution)/shard_map/all_to_all | solution.py:321
  107.5 36.3 %all-to-all-start.1 = ((bf16[8,256,256]{2,1,0:T(8,128)(2,1)}), bf16[8,256,256]{2,1,0:T(8,128)(2,1)S(1)}, u32[]{:S(2)}, u32[]{:S(2)}) async-start(bf16[8,256,256]{2,1,0:T(8,128)(2,1)} %get-tuple-element.24), calls=%async_computation.1 | async-start | bytes 2097152 | tf_op jit(solution)/shard_map/all_to_all | solution.py:321
  143.8 4.9 %copy-start = (bf16[8,256,256]{2,1,0:T(8,128)(2,1)}, bf16[8,256,256]{2,1,0:T(8,128)(2,1)S(1)}, u32[]{:S(2)}) copy-start(bf16[8,256,256]{2,1,0:T(8,128)(2,1)S(1)} %all-to-all-done.1.refs_1_) | copy-start | bytes 3145732
  143.8 54.3 %all-to-all-start.3 = ((bf16[8,256,256]{2,1,0:T(8,128)(2,1)}), bf16[8,256,256]{2,1,0:T(8,128)(2,1)S(1)}, u32[]{:S(2)}, u32[]{:S(2)}) async-start(bf16[8,256,256]{2,1,0:T(8,128)(2,1)} %get-tuple-element.29), calls=%async_computation.3 | async-start | bytes 2097152 | tf_op jit(solution)/shard_map/all_to_all | solution.py:321
  198.1 4.8 %copy-start.1 = (bf16[8,256,256]{2,1,0:T(8,128)(2,1)}, bf16[8,256,256]{2,1,0:T(8,128)(2,1)S(1)}, u32[]{:S(2)}) copy-start(bf16[8,256,256]{2,1,0:T(8,128)(2,1)S(1)} %all-to-all-done.3.refs_1_) | copy-start | bytes 3145732
  198.1 54.3 %all-to-all-start.4 = ((bf16[8,3,256,256]{3,2,1,0:T(8,128)(2,1)}), bf16[8,3,256,256]{3,2,1,0:T(8,128)(2,1)}, u32[]{:S(2)}, u32[]{:S(2)}) async-start(bf16[8,3,256,256]{3,2,1,0:T(8,128)(2,1)} %get-tuple-element.31), calls=%async_computation.4 | async-start | bytes 6291456 | tf_op jit(solution)/shard_map/all_to_all | solution.py:321
  252.4 42.1 %all-to-all-start.6 = ((bf16[8,3,256,256]{3,2,1,0:T(8,128)(2,1)}), bf16[8,3,256,256]{3,2,1,0:T(8,128)(2,1)S(1)}, u32[]{:S(2)}, u32[]{:S(2)}) async-start(bf16[8,3,256,256]{3,2,1,0:T(8,128)(2,1)} %get-tuple-element.37), calls=%async_computation.6 | async-start | bytes 6291456 | tf_op jit(solution)/shard_map/all_to_all | solution.py:321
  294.5 1.6 copy-start.6
  296.1 36.4 %all-to-all-start.5 = ((bf16[8,256,256]{2,1,0:T(8,128)(2,1)}), bf16[8,256,256]{2,1,0:T(8,128)(2,1)S(1)}, u32[]{:S(2)}, u32[]{:S(2)}) async-start(bf16[8,256,256]{2,1,0:T(8,128)(2,1)} %get-tuple-element.35), calls=%async_computation.5 | async-start | bytes 2097152 | tf_op jit(solution)/shard_map/all_to_all | solution.py:321
  332.5 4.9 %copy-start.2 = (bf16[8,256,256]{2,1,0:T(8,128)(2,1)}, bf16[8,256,256]{2,1,0:T(8,128)(2,1)S(1)}, u32[]{:S(2)}) copy-start(bf16[8,256,256]{2,1,0:T(8,128)(2,1)S(1)} %all-to-all-done.5.refs_1_) | copy-start | bytes 3145732
  332.5 43.1 %all-to-all-start.7 = ((bf16[8,256,256]{2,1,0:T(8,128)(2,1)}), bf16[8,256,256]{2,1,0:T(8,128)(2,1)S(1)}, u32[]{:S(2)}, u32[]{:S(2)}) async-start(bf16[8,256,256]{2,1,0:T(8,128)(2,1)} %get-tuple-element.40), calls=%async_computation.7 | async-start | bytes 2097152 | tf_op jit(solution)/shard_map/all_to_all | solution.py:321
  375.6 1.0 copy-start.3
  376.5 38.3 %copy-start.4 = (bf16[256,2048]{1,0:T(8,128)(2,1)S(1)}, bf16[256,2048]{1,0:T(8,128)(2,1)}, u32[]{:S(2)}) copy-start(bf16[256,2048]{1,0:T(8,128)(2,1)} %dense_2_10.2) | copy-start | bytes 3145732

commit v2 on v1

--- a/solution.py
+++ b/solution.py
@@ -30,7 +30,7 @@
     dst[...] = (x32 * r * g.astype(F32)).astype(BF16)
 
 
-def _dense_kernel(layer, mlp, qkv, *refs):
+def _dense_kernel(layer, mlp, qkv, joined, *refs):
     refs = list(refs)
     x_ref = refs.pop(0)
     if mlp:
@@ -39,6 +39,8 @@
     if qkv:
         g1_ref, cos_ref, sin_ref, wq, wk, wv = refs[:6]
         refs = refs[6:]
+    if joined:
+        refs.pop(0)
     if mlp:
         y_ref = refs.pop(0)
     if qkv:
@@ -134,9 +136,9 @@
         def _(i):
             t = b_2 + kk * i
             acc = None
+            slots = [ready(t + k) for k in range(kk)]
             for k in range(kk):
-                slot = ready(t + k)
-                r = jnp.dot(u_s[:, k * nk:(k + 1) * nk], wbuf[slot], preferred_element_type=F32)
+                r = jnp.dot(u_s[:, k * nk:(k + 1) * nk], wbuf[slots[k]], preferred_element_type=F32)
                 acc = r if acc is None else acc + r
             col = pl.ds(pl.multiple_of(i * TILE, TILE), TILE)
             y_ref[:, col] = (xm_s[:, col].astype(F32) + acc).astype(BF16)
@@ -151,9 +153,9 @@
         @pl.loop(0, nq)
         def _(i):
             t = b_q + 3 * i
+            slots = [ready(t + m) for m in range(3)]
             for m in range(3):
-                slot = ready(t + m)
-                r = jnp.dot(h_s[...], wbuf[slot], preferred_element_type=F32)
+                r = jnp.dot(h_s[...], wbuf[slots[m]], preferred_element_type=F32)
                 for a in range(TILE // HEAD):
                     z = r[:, a * HEAD:(a + 1) * HEAD]
                     if m < 2:
@@ -164,62 +166,135 @@
                 start(t + m + NBUF)
 
 
-def _dense(layer, x, o, tabs, w, ncp, mlp, qkv):
+def _dense(layer, half, x, o, tabs, w, ncp, mlp, qkv, y=None):
     g1, g2, wq, wk, wv, wo, w1, w3, w2 = w
-    rows, d = x.shape
+    rows = tabs[0].shape[0] // 2
+    d = x.shape[1]
     ff = w1.shape[2]
     width = wq.shape[2] // ncp
     anyspace = pl.BlockSpec(memory_space=pl.ANY)
     vmem = pl.BlockSpec(memory_space=pltpu.VMEM)
-    ins, specs = [x], [vmem]
+
+    def part(a):
+        return pl.BlockSpec((rows, a.shape[1]), lambda i: (half if a.shape[0] > rows else 0, 0))
+
+    def whole(a):
+        return pl.BlockSpec(a.shape, lambda i: (0,) * len(a.shape))
+
+    ins, specs = [x], [part(x)]
     outs, ospecs = [], []
     scratch = [pltpu.VMEM((rows, d), BF16), pltpu.VMEM((NBUF, d, TILE), BF16), pltpu.SemaphoreType.DMA((NBUF,))]
     flops = 0
-    if mlp:
-        ins += [o, g2[layer:layer + 1], wo, w1, w3, w2]
-        specs += [vmem, vmem] + [anyspace] * 4
-        outs.append(jax.ShapeDtypeStruct((rows, d), BF16))
-        ospecs.append(vmem)
+    alias = {}
+    if mlp:
+        g = g2[layer:layer + 1]
+        ins += [o, g, wo, w1, w3, w2]
+        specs += [whole(o), whole(g)] + [anyspace] * 4
+        outs.append(jax.ShapeDtypeStruct((rows if qkv else 2 * rows, d), BF16))
+        ospecs.append(part(outs[-1]))
         scratch += [pltpu.VMEM((rows, d), BF16), pltpu.VMEM((rows, ff), BF16)]
         flops += 2 * rows * d * (d + 3 * ff)
     if qkv:
-        ins += [g1[layer + 1:layer + 2], tabs[0], tabs[1], wq, wk, wv]
-        specs += [vmem] * 3 + [anyspace] * 3
+        g = g1[layer + 1:layer + 2]
+        ins += [g, tabs[0], tabs[1], wq, wk, wv]
+        specs += [whole(g), part(tabs[0]), part(tabs[1])] + [anyspace] * 3
         outs.append(jax.ShapeDtypeStruct((ncp, 3, rows, width), BF16))
-        ospecs.append(vmem)
+        ospecs.append(whole(outs[-1]))
         flops += 2 * rows * d * 3 * wq.shape[2]
+    if y is not None:
+        alias = {len(ins): 0}
+        ins.append(y)
+        specs.append(anyspace)
     return pl.pallas_call(
-        functools.partial(_dense_kernel, layer, mlp, qkv),
+        functools.partial(_dense_kernel, layer, mlp, qkv, y is not None),
+        grid=(1,),
         out_shape=outs,
         in_specs=specs,
         out_specs=ospecs,
         scratch_shapes=scratch,
-        compiler_params=pltpu.CompilerParams(vmem_limit_bytes=VMEM_LIMIT),
+        input_output_aliases=alias,
+        compiler_params=pltpu.CompilerParams(vmem_limit_bytes=VMEM_LIMIT, dimension_semantics=("arbitrary",)),
         cost_estimate=pl.CostEstimate(flops=flops, bytes_accessed=flops // rows, transcendentals=0),
-        name=f"dense_{layer + 1}_{int(mlp)}{int(qkv)}",
+        name=f"dense_{layer + 1}_{half}",
     )(*ins)
 
 
-def _attn_kernel(late, first, *refs):
+def _cache_kernel(first, ra_ref, rb_ref, *refs):
+    kc_ref, vc_ref, il_s = refs if first else refs[2:]
+    n = pl.program_id(0)
+    half = pl.num_programs(0) // 2
+    seg, width = ra_ref.shape[2], ra_ref.shape[3]
+    nh = width // HEAD
+
+    def write(ref, order):
+        for which, out in ((1, kc_ref), (2, vc_ref)):
+            for i in range(2):
+                src = ref[order[i], which]
+                for h in range(nh):
+                    il_s[which - 1, pl.ds(i * seg * nh + h, seg, stride=nh), :] = (
+                        src[:, h * HEAD:(h + 1) * HEAD].astype(F32))
+            out[0] = il_s[which - 1].astype(BF16)
+
+    @pl.when(n < half)
+    def _():
+        write(ra_ref, (0, 1))
+
+    @pl.when(n >= half)
+    def _():
+        write(rb_ref, (1, 0))
+
+
+def _cache(layer, layers, ra, rb, caches):
+    ncp, _, seg, width = ra.shape
+    nh = width // HEAD
+    npair = ncp // 2
+    rows = 2 * seg * nh
+    ins = [ra, rb]
+    specs = [pl.BlockSpec((2, 3, seg, width), lambda n: (jnp.minimum(n, npair - 1), 0, 0, 0)),
+             pl.BlockSpec((2, 3, seg, width), lambda n: (jnp.minimum(2 * npair - 1 - n, npair - 1), 0, 0, 0))]
+    alias = {}
+    if caches is not None:
+        alias = {2: 0, 3: 1}
+        ins += list(caches)
+        specs += [pl.BlockSpec(memory_space=pl.ANY)] * 2
+    cache = jax.ShapeDtypeStruct((layers, 2 * ncp * seg * nh, HEAD), BF16)
+    spec = pl.BlockSpec((1, rows, HEAD), lambda n: (layer, n, 0))
+    return pl.pallas_call(
+        functools.partial(_cache_kernel, caches is None),
+        grid=(2 * npair,),
+        out_shape=[cache, cache],
+        in_specs=specs,
+        out_specs=[spec, spec],
+        scratch_shapes=[pltpu.VMEM((2, rows, HEAD), F32)],
+        input_output_aliases=alias,
+        compiler_params=pltpu.CompilerParams(dimension_semantics=("arbitrary",)),
+        cost_estimate=pl.CostEstimate(flops=4 * 10 ** 9, bytes_accessed=10 * ncp * seg * width * 2,
+                                      transcendentals=0),
+        name=f"cache_{layer}",
+    )(*ins)
+
+
+def _attn_kernel(late, *refs):
     refs = list(refs)
     qkv_ref = refs.pop(0)
     pre_ref = refs.pop(0) if late else None
-    if not first:
-        refs = refs[2:]
-    o_ref, kc_ref, vc_ref, acc_s, m_s, il_s = refs
-    p = pl.program_id(0)
-    npair = qkv_ref.shape[0] // 2
+    out_ref, o_s, acc_s, m_s, send_sem, recv_sem = refs
+    me = lax.axis_index('cp')
+    step = pl.program_id(0)
+    ncp = qkv_ref.shape[0]
+    npair = ncp // 2
     seg, width = qkv_ref.shape[2], qkv_ref.shape[3]
     nh = width // HEAD
     bq = 2 * seg
     scale = HEAD ** -0.5 * math.log2(math.e)
-
-    for which, out in ((1, kc_ref), (2, vc_ref)):
-        for i in range(2):
-            src = qkv_ref[2 * p + (1 - i if late else i), which]
-            for h in range(nh):
-                il_s[pl.ds(i * seg * nh + h, seg, stride=nh), :] = src[:, h * HEAD:(h + 1) * HEAD].astype(F32)
-        out[0] = il_s[...].astype(BF16)
+    p = lax.rem(me // 2 + 1 + step, npair)
+    barrier = pltpu.get_barrier_semaphore()
+
+    @pl.when(step == 0)
+    def _():
+        for i in range(1, ncp):
+            pl.semaphore_signal(barrier, inc=1, device_id={'cp': lax.rem(me + i, ncp)},
+                                device_id_type=pl.DeviceIdType.MESH)
 
     ones = jnp.ones((bq, HEAD), BF16)
 
@@ -248,8 +323,9 @@
         m_s[h] = m
 
     def full(ref, j):
+        ss = [scores(ref, j, h) for h in range(nh)]
         for h in range(nh):
-            s = scores(ref, j, h)
+            s = ss[h]
             old = m_s[h]
             m = jnp.maximum(old, jnp.broadcast_to(jnp.max(s, axis=1, keepdims=True), (bq, HEAD)))
             pr = jnp.exp2((s - wide(m, bq // HEAD)) * scale).astype(BF16)
@@ -273,43 +349,61 @@
 
     for h in range(nh):
         o = (acc_s[h, :, :HEAD] / acc_s[h, :, HEAD:]).astype(BF16)
-        o_ref[:, :, h * HEAD:(h + 1) * HEAD] = o.reshape(2, seg, HEAD)
-
-
-def _attention(layer, layers, late, qkv, pre, caches):
+        o_s[pl.ds(2 * p, 2), :, h * HEAD:(h + 1) * HEAD] = o.reshape(2, seg, HEAD)
+
+    @pl.when(step == 0)
+    def _():
+        pl.semaphore_wait(barrier, ncp - 1)
+
+    def remote(j, slot):
+        return pltpu.make_async_remote_copy(
+            src_ref=o_s.at[j], dst_ref=out_ref.at[slot], send_sem=send_sem.at[j], recv_sem=recv_sem.at[slot],
+            device_id={'cp': j}, device_id_type=pl.DeviceIdType.MESH)
+
+    def local():
+        return pltpu.make_async_copy(o_s.at[me], out_ref.at[me], recv_sem.at[me])
+
+    for a in range(2):
+        j = 2 * p + a
+
+        @pl.when(j != me)
+        def _():
+            remote(j, me).start()
+
+        @pl.when(j == me)
+        def _():
+            local().start()
+
+    @pl.when(step == npair - 1)
+    def _():
+        local().wait()
+        for i in range(1, ncp):
+            j = lax.rem(me + i, ncp)
+            remote(j, me).wait_send()
+            remote(j, j).wait_recv()
+
+
+def _attention(layer, late, qkv, pre):
     ncp, _, seg, width = qkv.shape
     nh = width // HEAD
     npair = ncp // 2
-    rows = 2 * seg * nh
     whole = pl.BlockSpec((ncp, 3, seg, width), lambda p: (0, 0, 0, 0))
-    ins, specs = [qkv], [whole]
-    if late:
-        ins.append(pre)
-        specs.append(whole)
-    alias = {}
-    if caches is not None:
-        alias = {len(ins): 1, len(ins) + 1: 2}
-        ins += list(caches)
-        specs += [pl.BlockSpec(memory_space=pl.ANY)] * 2
-    where = (lambda p: (layer, 2 * npair - 1 - p, 0)) if late else (lambda p: (layer, p, 0))
-    cache = jax.ShapeDtypeStruct((layers, 2 * ncp * seg * nh, HEAD), BF16)
     pairs = (ncp * seg) ** 2 // 2 * (3 if late else 1) * nh
-    o, kc, vc = pl.pallas_call(
-        functools.partial(_attn_kernel, late, caches is None),
+    return pl.pallas_call(
+        functools.partial(_attn_kernel, late),
         grid=(npair,),
-        out_shape=[jax.ShapeDtypeStruct((ncp, seg, width), BF16), cache, cache],
-        in_specs=specs,
-        out_specs=[pl.BlockSpec((2, seg, width), lambda p: (p, 0, 0)),
-                   pl.BlockSpec((1, rows, HEAD), where), pl.BlockSpec((1, rows, HEAD), where)],
-        scratch_shapes=[pltpu.VMEM((nh, 2 * seg, 2 * HEAD), F32), pltpu.VMEM((nh, 2 * seg, HEAD), F32),
-                        pltpu.VMEM((rows, HEAD), F32)],
-        input_output_aliases=alias,
-        compiler_params=pltpu.CompilerParams(vmem_limit_bytes=VMEM_LIMIT, dimension_semantics=("arbitrary",)),
+        out_shape=jax.ShapeDtypeStruct((ncp, seg, width), BF16),
+        in_specs=[whole] * (2 if late else 1),
+        out_specs=pl.BlockSpec(memory_space=pl.ANY),
+        scratch_shapes=[pltpu.VMEM((ncp, seg, width), BF16),
+                        pltpu.VMEM((nh, 2 * seg, 2 * HEAD), F32), pltpu.VMEM((nh, 2 * seg, HEAD), F32),
+                        pltpu.SemaphoreType.DMA((ncp,)), pltpu.SemaphoreType.DMA((ncp,))],
+        compiler_params=pltpu.CompilerParams(vmem_limit_bytes=VMEM_LIMIT, dimension_semantics=("arbitrary",),
+                                             collective_id=2 * layer + int(late), has_side_effects=True),
         cost_estimate=pl.CostEstimate(flops=pairs * HEAD * 8, bytes_accessed=8 * ncp * seg * width * 2,
                                       transcendentals=pairs),
         name=f"attn_{layer}_{int(late)}",
-    )(*ins)
-    return o, (kc, vc)
+    )(*((qkv, pre) if late else (qkv,)))
 
 
 def solution(mesh):
@@ -320,29 +414,30 @@
     def swap(a):
         return lax.all_to_all(a, 'cp', 0, 0, tiled=True)
 
+    def after(a, *deps):
+        return lax.optimization_barrier((a,) + deps)[0]
+
     def body(x, pos, g1, g2, wq, wk, wv, wo, w1, w3, w2):
         w = (g1, g2, wq, wk, wv, wo, w1, w3, w2)
         layers = wq.shape[0]
-        seg = x.shape[0] // 2
-        cos, sin = _tables(pos)
-        tabs = [(cos[:seg], sin[:seg]), (cos[seg:], sin[seg:])]
-        xs = [x[:seg], x[seg:]]
-        qkv = [_dense(-1, xs[i], None, tabs[i], w, ncp, False, True)[0] for i in range(2)]
+        tabs = _tables(pos)
+        xs = [x, x]
+        qkv = [_dense(-1, i, x, None, tabs, w, ncp, False, True)[0] for i in range(2)]
         caches = None
         for l in range(layers):
             more = l + 1 < layers
             ra = swap(qkv[0])
-            qb, ra = lax.optimization_barrier((qkv[1], ra))
-            rb = swap(qb)
-            oa, caches = _attention(l, layers, False, ra, None, caches)
-            res = _dense(l, xs[0], swap(oa), tabs[0], w, ncp, True, more)
-            ob, caches = _attention(l, layers, True, rb, ra, caches)
-            res_b = _dense(l, xs[1], swap(ob), tabs[1], w, ncp, True, more)
+            rb = swap(after(qkv[1], ra))
+            oa = _attention(l, False, ra, None)
+            res = _dense(l, 0, xs[0], oa, tabs, w, ncp, True, more)
+            ob = _attention(l, True, after(rb, res[0]), ra)
+            caches = _cache(l, layers, ra, rb, caches)
+            res_b = _dense(l, 1, xs[1], ob, tabs, w, ncp, True, more, None if more else res[0])
             xs = [res[0], res_b[0]]
             if more:
                 qkv = [res[1], res_b[1]]
         kc, vc = (a.reshape(layers, -1, wq.shape[2] // ncp // HEAD, HEAD) for a in caches)
-        return jnp.concatenate(xs, axis=0), kc, vc
+        return xs[1], kc, vc
 
     return jax.shard_map(body, mesh=mesh, in_specs=(act, P(('req', 'cp'))) + (P(),) * 9,
                          out_specs=(act, cache, cache), check_vma=False)

time: 419 us -> 439 us (1.048)
  Pallas kernels: 295 us -> 389 us
  waiting for transfers between devices: 69.2 us -> 23.2 us
  starting transfers between devices: 40.2 us -> 20.3 us
  local copies, waits for them, and re-layouts: 6.98 us -> 2.02 us
    pallas_call x10 -> x12, Pallas kernels: 295 us -> 389 us  [the longest x6 200 us: _dense(): pl.pallas_call(functools.partial(_dense_kernel, layer, mlp, qkv, y is not...]
    all_to_all x8 -> x4, waiting for transfers between devices: 69.2 us -> 23.2 us  [swap(): return lax.all_to_all(a, 'cp', 0, 0, tiled=True)]
    all_to_all x8 -> x4, starting transfers between devices: 40.2 us -> 20.3 us  [swap(): return lax.all_to_all(a, 'cp', 0, 0, tiled=True)]
  transfers between devices with their start and end apart: 8 -> 4, of which waited for: 3 -> 1; matrix products, arithmetic and copies ran while one was open for 0% -> 0% of each run, Pallas kernels for 58% -> 68%
where the time goes in v2:
time: 439 us; the launch traced here: 438 us
  Pallas kernels  389 us (89%)
  waiting for transfers between devices  23.2 us (5%)
  starting transfers between devices  20.3 us (5%)
    pallas_call x6, Pallas kernels, _dense(): pl.pallas_call(functools.partial(_dense_kernel, layer, mlp, qkv, y is not...  200 us
    pallas_call x4, Pallas kernels, _attention(): pl.pallas_call(functools.partial(_attn_kernel, late), grid=(npair,), out_...  172 us
    all_to_all x4, waiting for transfers between devices, swap(): return lax.all_to_all(a, 'cp', 0, 0, tiled=True)  23.2 us
    all_to_all x4, starting transfers between devices, swap(): return lax.all_to_all(a, 'cp', 0, 0, tiled=True)  20.3 us
    pallas_call x2, Pallas kernels, _cache(): pl.pallas_call(functools.partial(_cache_kernel, caches is None), grid=(2...  15.7 us
  transfers between devices with their start and end apart: 4, of which 1 were waited for; matrix products, arithmetic and copies ran while one was open for 0% of the time, Pallas kernels for 68%

profile of v2, /device:TPU:81, one launch (start us, length us, event | category | flops | bytes accessed | tf_op | source)
XLA Modules:
  0.0 437.6 jit_solution(1109986979403726238)
XLA Ops:
  0.6 1.4 fusion.2
  2.0 0.7 convert_element_type.3
  2.7 1.0 fusion
  3.7 1.0 pad_maximum_fusion
  4.7 13.5 %dense_0_0.1 = bf16[8,3,256,256]{3,2,1,0:T(8,128)(2,1)} custom-call(bf16[512,2048]{1,0:T(8,128)(2,1)} %refs_0_.7, bf16[1,2048]{1,0:T(2,128)(2,1)} %get-tuple-element.30.refs_1_, f32[512,128]{1,0:T(8,128)} %get-tuple-element.34.refs_2_.refs_8_, f32[512,128]{1,0:T(8,128)} %get-tuple-element.35.refs_3_.refs_9_, bf16[2,2048,2048]{2,1,0:T(8,128)(2,1)} %refs_10_.3, ...), custom_call_target="tpu_custom_call" | custom-call | flops 6442450944 | bytes 25165824 | tf_op jit(solution)/shard_map/dense_0_0/pallas_call | solution.py:208
  18.2 0.0 copy-start.2
  18.2 6.0 %all-to-all-start = ((bf16[8,3,256,256]{3,2,1,0:T(8,128)(2,1)}), bf16[8,3,256,256]{3,2,1,0:T(8,128)(2,1)S(1)}, u32[]{:S(2)}, u32[]{:S(2)}) async-start(bf16[8,3,256,256]{3,2,1,0:T(8,128)(2,1)} %dense_0_0.1), calls=%async_computation | async-start | bytes 6291456 | tf_op jit(solution)/shard_map/all_to_all | solution.py:415
  24.2 0.0 copy-done.2
  24.2 0.6 fusion.1
  24.8 13.5 %dense_0_1.1 = bf16[8,3,256,256]{3,2,1,0:T(8,128)(2,1)} custom-call(bf16[512,2048]{1,0:T(8,128)(2,1)} %refs_0_.7, bf16[1,2048]{1,0:T(2,128)(2,1)} %get-tuple-element.30.refs_1_, f32[512,128]{1,0:T(8,128)} %get-tuple-element.34.refs_2_.refs_8_, f32[512,128]{1,0:T(8,128)} %get-tuple-element.35.refs_3_.refs_9_, bf16[2,2048,2048]{2,1,0:T(8,128)(2,1)} %refs_10_.3, ...), custom_call_target="tpu_custom_call" | custom-call | flops 6442450944 | bytes 25165824 | tf_op jit(solution)/shard_map/dense_0_1/pallas_call | solution.py:208
  38.3 23.1 %all-to-all-done.refs_0_.refs_1_.ra_ref = bf16[8,3,256,256]{3,2,1,0:T(8,128)(2,1)S(1)} async-done(((bf16[8,3,256,256]{3,2,1,0:T(8,128)(2,1)}), bf16[8,3,256,256]{3,2,1,0:T(8,128)(2,1)S(1)}, u32[]{:S(2)}, u32[]{:S(2)}) %all-to-all-start) | async-done | bytes 3145760 | tf_op jit(solution)/shard_map/all_to_all | solution.py:415
  61.4 0.0 copy-start
  61.4 5.5 %all-to-all-start.1 = ((bf16[8,3,256,256]{3,2,1,0:T(8,128)(2,1)}), bf16[8,3,256,256]{3,2,1,0:T(8,128)(2,1)}, u32[]{:S(2)}, u32[]{:S(2)}) async-start(bf16[8,3,256,256]{3,2,1,0:T(8,128)(2,1)} %dense_0_1.1), calls=%async_computation.1 | async-start | bytes 6291456 | tf_op jit(solution)/shard_map/all_to_all | solution.py:415
  67.0 0.0 copy-done
  67.0 49.2 %attn_0_0.1.refs_1_ = bf16[8,256,256]{2,1,0:T(8,128)(2,1)} custom-call(bf16[8,3,256,256]{3,2,1,0:T(8,128)(2,1)} %copy-done), custom_call_target="tpu_custom_call" | custom-call | flops 4294967296 | bytes 8388608 | tf_op jit(solution)/shard_map/attn_0_0/pallas_call | solution.py:392
  116.2 47.8 %dense_1_0.1 = (bf16[256,2048]{1,0:T(8,128)(2,1)}, bf16[8,3,256,256]{3,2,1,0:T(8,128)(2,1)}) custom-call(bf16[512,2048]{1,0:T(8,128)(2,1)} %refs_0_.7, bf16[8,256,256]{2,1,0:T(8,128)(2,1)} %attn_0_0.1.refs_1_, bf16[1,2048]{1,0:T(2,128)(2,1)} %get-tuple-element.28.refs_2_, bf16[2,2048,2048]{2,1,0:T(8,128)(2,1)} %refs_3_.7, bf16[2,2048,8192]{2,1,0:T(8,128)(2,1)} %refs_4_.11, ...), custom_call_target="tpu_custom_call" | custom-call | flops 34359738368 | bytes 134217728 | tf_op jit(solution)/shard_map/dense_1_0/pallas_call | solution.py:208
  164.0 0.0 all-to-all-done.1.refs_0_.rb_ref
  164.0 4.0 all-to-all-start.2
  168.0 47.6 %attn_0_1.1.refs_1_ = bf16[8,256,256]{2,1,0:T(8,128)(2,1)} custom-call(bf16[8,3,256,256]{3,2,1,0:T(8,128)(2,1)} %all-to-all-done.1.refs_0_.rb_ref, bf16[8,3,256,256]{3,2,1,0:T(8,128)(2,1)} %copy-done), custom_call_target="tpu_custom_call" | custom-call | flops 12884901888 | bytes 8388608 | tf_op jit(solution)/shard_map/attn_0_1/pallas_call | solution.py:392
  215.6 47.8 %dense_1_1.1 = (bf16[256,2048]{1,0:T(8,128)(2,1)}, bf16[8,3,256,256]{3,2,1,0:T(8,128)(2,1)}) custom-call(bf16[512,2048]{1,0:T(8,128)(2,1)} %refs_0_.7, bf16[8,256,256]{2,1,0:T(8,128)(2,1)} %attn_0_1.1.refs_1_, bf16[1,2048]{1,0:T(2,128)(2,1)} %get-tuple-element.28.refs_2_, bf16[2,2048,2048]{2,1,0:T(8,128)(2,1)} %refs_3_.7, bf16[2,2048,8192]{2,1,0:T(8,128)(2,1)} %refs_4_.11, ...), custom_call_target="tpu_custom_call" | custom-call | flops 34359738368 | bytes 134217728 | tf_op jit(solution)/shard_map/dense_1_1/pallas_call | solution.py:208
  263.4 0.0 all-to-all-done.2.refs_0_.refs_1_.ra_ref
  263.4 0.0 copy-start.1
  263.5 4.8 %all-to-all-start.3 = ((bf16[8,3,256,256]{3,2,1,0:T(8,128)(2,1)}), bf16[8,3,256,256]{3,2,1,0:T(8,128)(2,1)}, u32[]{:S(2)}, u32[]{:S(2)}) async-start(bf16[8,3,256,256]{3,2,1,0:T(8,128)(2,1)} %get-tuple-element.21), calls=%async_computation.3 | async-start | bytes 6291456 | tf_op jit(solution)/shard_map/all_to_all | solution.py:415
  268.2 0.0 copy-done.1
  268.2 47.0 %attn_1_0.1.refs_1_ = bf16[8,256,256]{2,1,0:T(8,128)(2,1)} custom-call(bf16[8,3,256,256]{3,2,1,0:T(8,128)(2,1)} %copy-done.1), custom_call_target="tpu_custom_call" | custom-call | flops 4294967296 | bytes 8388608 | tf_op jit(solution)/shard_map/attn_1_0/pallas_call | solution.py:392
  315.3 7.8 %cache_0.1 = (bf16[2,8192,128]{2,1,0:T(8,128)(2,1)}, bf16[2,8192,128]{2,1,0:T(8,128)(2,1)}) custom-call(bf16[8,3,256,256]{3,2,1,0:T(8,128)(2,1)} %copy-done, bf16[8,3,256,256]{3,2,1,0:T(8,128)(2,1)} %all-to-all-done.1.refs_0_.rb_ref), custom_call_target="tpu_custom_call" | custom-call | flops 4000000000 | bytes 10485760 | tf_op jit(solution)/shard_map/cache_0/pallas_call | solution.py:262
  323.1 39.0 %dense_2_0.1.refs_7_ = bf16[512,2048]{1,0:T(8,128)(2,1)} custom-call(bf16[256,2048]{1,0:T(8,128)(2,1)} %get-tuple-element.16.refs_0_, bf16[8,256,256]{2,1,0:T(8,128)(2,1)} %attn_1_0.1.refs_1_, bf16[1,2048]{1,0:T(2,128)(2,1)} %get-tuple-element.27.refs_2_, bf16[2,2048,2048]{2,1,0:T(8,128)(2,1)} %refs_3_.7, bf16[2,2048,8192]{2,1,0:T(8,128)(2,1)} %refs_4_.11, ...), custom_call_target="tpu_custom_call" | custom-call | flops 27917287424 | bytes 109051904 | tf_op jit(solution)/shard_map/dense_2_0/pallas_call | solution.py:208
  362.1 0.0 all-to-all-done.3.refs_0_.rb_ref
  362.1 28.6 %attn_1_1.1.refs_1_ = bf16[8,256,256]{2,1,0:T(8,128)(2,1)} custom-call(bf16[8,3,256,256]{3,2,1,0:T(8,128)(2,1)} %all-to-all-done.3.refs_0_.rb_ref, bf16[8,3,256,256]{3,2,1,0:T(8,128)(2,1)} %copy-done.1), custom_call_target="tpu_custom_call" | custom-call | flops 12884901888 | bytes 8388608 | tf_op jit(solution)/shard_map/attn_1_1/pallas_call | solution.py:392
  390.7 39.0 %dense_2_1.1 = bf16[512,2048]{1,0:T(8,128)(2,1)} custom-call(bf16[256,2048]{1,0:T(8,128)(2,1)} %get-tuple-element.18.refs_0_, bf16[8,256,256]{2,1,0:T(8,128)(2,1)} %attn_1_1.1.refs_1_, bf16[1,2048]{1,0:T(2,128)(2,1)} %get-tuple-element.27.refs_2_, bf16[2,2048,2048]{2,1,0:T(8,128)(2,1)} %refs_3_.7, ...), custom_call_target="tpu_custom_call", output_to_operand_aliasing={{}: (7, {})} | custom-call | flops 27917287424 | bytes 109051904 | tf_op jit(solution)/shard_map/dense_2_1/pallas_call | solution.py:208
  429.7 7.8 %cache_1.1 = (bf16[2,8192,128]{2,1,0:T(8,128)(2,1)}, bf16[2,8192,128]{2,1,0:T(8,128)(2,1)}) custom-call(bf16[8,3,256,256]{3,2,1,0:T(8,128)(2,1)} %copy-done.1, bf16[8,3,256,256]{3,2,1,0:T(8,128)(2,1)} %all-to-all-done.3.refs_0_.rb_ref, bf16[2,8192,128]{2,1,0:T(8,128)(2,1)} %get-tuple-element.23.refs_0_, ...), custom_call_target="tpu_custom_call", output_to_operand_aliasing={{0}: (2, {}), {1}: (3, {})} | custom-call | flops 4000000000 | bytes 10485760 | tf_op jit(solution)/shard_map/cache_1/pallas_call | solution.py:262
  (1 shorter events, 0.0 us)
Async XLA Ops:
  18.2 6.0 %copy-start.2 = (bf16[2,2048]{1,0:T(2,128)(2,1)S(1)}, bf16[2,2048]{1,0:T(2,128)(2,1)}, u32[]{:S(2)}) copy-start(bf16[2,2048]{1,0:T(2,128)(2,1)} %param.14) | copy-start | bytes 24580
  18.2 43.3 %all-to-all-start = ((bf16[8,3,256,256]{3,2,1,0:T(8,128)(2,1)}), bf16[8,3,256,256]{3,2,1,0:T(8,128)(2,1)S(1)}, u32[]{:S(2)}, u32[]{:S(2)}) async-start(bf16[8,3,256,256]{3,2,1,0:T(8,128)(2,1)} %dense_0_0.1), calls=%async_computation | async-start | bytes 6291456 | tf_op jit(solution)/shard_map/all_to_all | solution.py:415
  61.4 5.5 %copy-start = (bf16[8,3,256,256]{3,2,1,0:T(8,128)(2,1)}, bf16[8,3,256,256]{3,2,1,0:T(8,128)(2,1)S(1)}, u32[]{:S(2)}) copy-start(bf16[8,3,256,256]{3,2,1,0:T(8,128)(2,1)S(1)} %all-to-all-done.refs_0_.refs_1_.ra_ref) | copy-start | bytes 9437188
  61.4 102.6 %all-to-all-start.1 = ((bf16[8,3,256,256]{3,2,1,0:T(8,128)(2,1)}), bf16[8,3,256,256]{3,2,1,0:T(8,128)(2,1)}, u32[]{:S(2)}, u32[]{:S(2)}) async-start(bf16[8,3,256,256]{3,2,1,0:T(8,128)(2,1)} %dense_0_1.1), calls=%async_computation.1 | async-start | bytes 6291456 | tf_op jit(solution)/shard_map/all_to_all | solution.py:415
  164.0 99.4 %all-to-all-start.2 = ((bf16[8,3,256,256]{3,2,1,0:T(8,128)(2,1)}), bf16[8,3,256,256]{3,2,1,0:T(8,128)(2,1)S(1)}, u32[]{:S(2)}, u32[]{:S(2)}) async-start(bf16[8,3,256,256]{3,2,1,0:T(8,128)(2,1)} %get-tuple-element.20), calls=%async_computation.2 | async-start | bytes 6291456 | tf_op jit(solution)/shard_map/all_to_all | solution.py:415
  263.4 4.8 %copy-start.1 = (bf16[8,3,256,256]{3,2,1,0:T(8,128)(2,1)}, bf16[8,3,256,256]{3,2,1,0:T(8,128)(2,1)S(1)}, u32[]{:S(2)}) copy-start(bf16[8,3,256,256]{3,2,1,0:T(8,128)(2,1)S(1)} %all-to-all-done.2.refs_0_.refs_1_.ra_ref) | copy-start | bytes 9437188
  263.5 98.7 %all-to-all-start.3 = ((bf16[8,3,256,256]{3,2,1,0:T(8,128)(2,1)}), bf16[8,3,256,256]{3,2,1,0:T(8,128)(2,1)}, u32[]{:S(2)}, u32[]{:S(2)}) async-start(bf16[8,3,256,256]{3,2,1,0:T(8,128)(2,1)} %get-tuple-element.21), calls=%async_computation.3 | async-start | bytes 6291456 | tf_op jit(solution)/shard_map/all_to_all | solution.py:415

commit v3 on v2

--- a/solution.py
+++ b/solution.py
@@ -11,6 +11,7 @@
 HEAD = 128
 TILE = 512
 NBUF = 8
+RING = 14
 F32 = jnp.float32
 BF16 = jnp.bfloat16
 VMEM_LIMIT = 60 * 1024 * 1024
@@ -219,17 +220,17 @@
     )(*ins)
 
 
-def _cache_kernel(first, ra_ref, rb_ref, *refs):
+def _cache_kernel(first, ka_ref, va_ref, kb_ref, vb_ref, *refs):
     kc_ref, vc_ref, il_s = refs if first else refs[2:]
     n = pl.program_id(0)
     half = pl.num_programs(0) // 2
-    seg, width = ra_ref.shape[2], ra_ref.shape[3]
+    seg, width = ka_ref.shape[2], ka_ref.shape[3]
     nh = width // HEAD
 
-    def write(ref, order):
+    def write(pair, order):
         for which, out in ((1, kc_ref), (2, vc_ref)):
             for i in range(2):
-                src = ref[order[i], which]
+                src = pair[which - 1][order[i], 0]
                 for h in range(nh):
                     il_s[which - 1, pl.ds(i * seg * nh + h, seg, stride=nh), :] = (
                         src[:, h * HEAD:(h + 1) * HEAD].astype(F32))
@@ -237,11 +238,11 @@
 
     @pl.when(n < half)
     def _():
-        write(ra_ref, (0, 1))
+        write((ka_ref, va_ref), (0, 1))
 
     @pl.when(n >= half)
     def _():
-        write(rb_ref, (1, 0))
+        write((kb_ref, vb_ref), (1, 0))
 
 
 def _cache(layer, layers, ra, rb, caches):
@@ -249,12 +250,13 @@
     nh = width // HEAD
     npair = ncp // 2
     rows = 2 * seg * nh
-    ins = [ra, rb]
-    specs = [pl.BlockSpec((2, 3, seg, width), lambda n: (jnp.minimum(n, npair - 1), 0, 0, 0)),
-             pl.BlockSpec((2, 3, seg, width), lambda n: (jnp.minimum(2 * npair - 1 - n, npair - 1), 0, 0, 0))]
+    ins = [ra, ra, rb, rb]
+    block = (2, 1, seg, width)
+    specs = [pl.BlockSpec(block, lambda n, m=m: (jnp.minimum(n, npair - 1), m, 0, 0)) for m in (1, 2)]
+    specs += [pl.BlockSpec(block, lambda n, m=m: (jnp.minimum(2 * npair - 1 - n, npair - 1), m, 0, 0)) for m in (1, 2)]
     alias = {}
     if caches is not None:
-        alias = {2: 0, 3: 1}
+        alias = {4: 0, 5: 1}
         ins += list(caches)
         specs += [pl.BlockSpec(memory_space=pl.ANY)] * 2
     cache = jax.ShapeDtypeStruct((layers, 2 * ncp * seg * nh, HEAD), BF16)
@@ -274,27 +276,83 @@
     )(*ins)
 
 
-def _attn_kernel(late, *refs):
+def _layer_kernel(layer, late, more, swap, joined, *refs):
     refs = list(refs)
-    qkv_ref = refs.pop(0)
+    x_ref, qkv_ref = refs[:2]
+    refs = refs[2:]
     pre_ref = refs.pop(0) if late else None
-    out_ref, o_s, acc_s, m_s, send_sem, recv_sem = refs
-    me = lax.axis_index('cp')
-    step = pl.program_id(0)
-    ncp = qkv_ref.shape[0]
+    g2_ref, wo, w1, w3, w2 = refs[:5]
+    refs = refs[5:]
+    if more:
+        g1_ref, cos_ref, sin_ref, wq, wk, wv = refs[:6]
+        refs = refs[6:]
+    if swap:
+        ex_in = refs.pop(0)
+    if joined:
+        refs.pop(0)
+    y_ref = refs.pop(0)
+    if more:
+        nxt_ref = refs.pop(0)
+    if swap:
+        ex_out = refs.pop(0)
+    h_s, wbuf, sems, xm_s, u_s, o_s, o_r, acc_s, m_s, send_sem, recv_sem, out_sem = refs[:12]
+    if swap:
+        xs_sem, xr_sem = refs[12:]
+    nbuf = wbuf.shape[0]
+    half = int(late)
+    rows, d = h_s.shape
+    nk = wbuf.shape[1]
+    ncp, _, seg, width = qkv_ref.shape
     npair = ncp // 2
-    seg, width = qkv_ref.shape[2], qkv_ref.shape[3]
     nh = width // HEAD
     bq = 2 * seg
     scale = HEAD ** -0.5 * math.log2(math.e)
-    p = lax.rem(me // 2 + 1 + step, npair)
+    me = lax.axis_index('cp')
     barrier = pltpu.get_barrier_semaphore()
-
-    @pl.when(step == 0)
-    def _():
-        for i in range(1, ncp):
-            pl.semaphore_signal(barrier, inc=1, device_id={'cp': lax.rem(me + i, ncp)},
-                                device_id_type=pl.DeviceIdType.MESH)
+    for i in range(1, ncp):
+        pl.semaphore_signal(barrier, inc=1, device_id={'cp': lax.rem(me + i, ncp)},
+                            device_id_type=pl.DeviceIdType.MESH)
+
+    def col(i):
+        return pl.ds(i * TILE, TILE)
+
+    no, nf = wo.shape[2] // TILE, w1.shape[2] // TILE
+    kk, ny = w2.shape[1] // nk, w2.shape[2] // TILE
+    b_o, b_1, b_2 = 0, no, no + 2 * nf
+    b_q = b_2 + ny * kk
+    segs = [(b_o, no, lambda i: [wo.at[layer, :, col(i)]]),
+            (b_1, 2 * nf, lambda i: [w1.at[layer, :, col(i // 2)], w3.at[layer, :, col(i // 2)]]),
+            (b_2, ny * kk, lambda i: [w2.at[layer, pl.ds((i % kk) * nk, nk), col(i // kk)]])]
+    if more:
+        nq = wq.shape[2] // TILE
+        segs.append((b_q, 3 * nq, lambda i: [w.at[layer + 1, :, col(i // 3)] for w in (wq, wk, wv)]))
+
+    def start(t):
+        slot = t % nbuf if isinstance(t, int) else lax.rem(t, nbuf)
+        for first, n, srcs in segs:
+            if isinstance(t, int):
+                if first <= t < first + n:
+                    lst = srcs(t - first)
+                    pltpu.make_async_copy(lst[(t - first) % len(lst)], wbuf.at[slot], sems.at[slot]).start()
+                continue
+            i = t - first
+            lst = srcs(i)
+            for which, src in enumerate(lst):
+                cond = (t >= first) & (t < first + n)
+                if len(lst) > 1:
+                    cond = cond & (lax.rem(i, len(lst)) == which)
+
+                @pl.when(cond)
+                def _(src=src):
+                    pltpu.make_async_copy(src, wbuf.at[slot], sems.at[slot]).start()
+
+    def ready(t):
+        slot = lax.rem(t, nbuf)
+        pltpu.make_async_copy(wo.at[layer, :, col(0)], wbuf.at[slot], sems.at[slot]).wait()
+        return slot
+
+    for t in range(nbuf):
+        start(t)
 
     ones = jnp.ones((bq, HEAD), BF16)
 
@@ -304,106 +362,224 @@
     def wide(a, n):
         return jnp.concatenate([a] * n, axis=1)
 
-    def scores(ref, j, h):
-        return lax.dot_general(block(qkv_ref, p, 0, h), block(ref, j, 1, h), (((1,), (1,)), ((), ())),
-                               preferred_element_type=F32)
-
-    r = lax.broadcasted_iota(jnp.int32, (bq, bq), 0)
-    c = lax.broadcasted_iota(jnp.int32, (bq, bq), 1)
-    if late:
-        r = jnp.where(r < seg, r + seg, r - seg)
-        c = jnp.where(c < seg, c + seg, c - seg)
-    mask = c <= r
-    for h in range(nh):
-        s = jnp.where(mask, scores(qkv_ref, p, h), -jnp.inf)
-        m = jnp.broadcast_to(jnp.max(s, axis=1, keepdims=True), (bq, HEAD))
-        pr = jnp.exp2((s - wide(m, bq // HEAD)) * scale).astype(BF16)
-        v = jnp.concatenate([block(qkv_ref, p, 2, h), ones], axis=1)
-        acc_s[h] = jnp.dot(pr, v, preferred_element_type=F32)
-        m_s[h] = m
-
-    def full(ref, j):
-        ss = [scores(ref, j, h) for h in range(nh)]
-        for h in range(nh):
-            s = ss[h]
-            old = m_s[h]
-            m = jnp.maximum(old, jnp.broadcast_to(jnp.max(s, axis=1, keepdims=True), (bq, HEAD)))
-            pr = jnp.exp2((s - wide(m, bq // HEAD)) * scale).astype(BF16)
-            v = jnp.concatenate([block(ref, j, 2, h), ones], axis=1)
-            alpha = jnp.exp2((old - m) * scale)
-            acc_s[h] = acc_s[h] * wide(alpha, 2) + jnp.dot(pr, v, preferred_element_type=F32)
-            m_s[h] = m
-
-    if late:
-        @pl.loop(0, npair)
-        def _(j):
-            full(pre_ref, j)
-
-        @pl.loop(p + 1, npair)
-        def _(j):
-            full(qkv_ref, j)
-    else:
-        @pl.loop(0, p)
-        def _(j):
-            full(qkv_ref, j)
-
-    for h in range(nh):
-        o = (acc_s[h, :, :HEAD] / acc_s[h, :, HEAD:]).astype(BF16)
-        o_s[pl.ds(2 * p, 2), :, h * HEAD:(h + 1) * HEAD] = o.reshape(2, seg, HEAD)
-
-    @pl.when(step == 0)
-    def _():
-        pl.semaphore_wait(barrier, ncp - 1)
-
     def remote(j, slot):
         return pltpu.make_async_remote_copy(
-            src_ref=o_s.at[j], dst_ref=out_ref.at[slot], send_sem=send_sem.at[j], recv_sem=recv_sem.at[slot],
+            src_ref=o_s.at[j], dst_ref=o_r.at[slot], send_sem=send_sem.at[j], recv_sem=recv_sem.at[slot],
             device_id={'cp': j}, device_id_type=pl.DeviceIdType.MESH)
 
     def local():
-        return pltpu.make_async_copy(o_s.at[me], out_ref.at[me], recv_sem.at[me])
-
-    for a in range(2):
-        j = 2 * p + a
-
-        @pl.when(j != me)
+        return pltpu.make_async_copy(o_s.at[me], o_r.at[me], recv_sem.at[me])
+
+    @pl.loop(0, npair)
+    def _(step):
+        p = lax.rem(me // 2 + 1 + step, npair)
+
+        def scores(ref, j, h):
+            return lax.dot_general(block(qkv_ref, p, 0, h), block(ref, j, 1, h), (((1,), (1,)), ((), ())),
+                                   preferred_element_type=F32)
+
+        r = lax.broadcasted_iota(jnp.int32, (bq, bq), 0)
+        c = lax.broadcasted_iota(jnp.int32, (bq, bq), 1)
+        if late:
+            r = jnp.where(r < seg, r + seg, r - seg)
+            c = jnp.where(c < seg, c + seg, c - seg)
+        mask = c <= r
+        for h in range(nh):
+            s = jnp.where(mask, scores(qkv_ref, p, h), -jnp.inf)
+            m = jnp.broadcast_to(jnp.max(s, axis=1, keepdims=True), (bq, HEAD))
+            pr = jnp.exp2((s - wide(m, bq // HEAD)) * scale).astype(BF16)
+            v = jnp.concatenate([block(qkv_ref, p, 2, h), ones], axis=1)
+            acc_s[h] = jnp.dot(pr, v, preferred_element_type=F32)
+            m_s[h] = m
+
+        def full(ref, j):
+            ss = [scores(ref, j, h) for h in range(nh)]
+            for h in range(nh):
+                s = ss[h]
+                old = m_s[h]
+                m = jnp.maximum(old, jnp.broadcast_to(jnp.max(s, axis=1, keepdims=True), (bq, HEAD)))
+                pr = jnp.exp2((s - wide(m, bq // HEAD)) * scale).astype(BF16)
+                v = jnp.concatenate([block(ref, j, 2, h), ones], axis=1)
+                alpha = jnp.exp2((old - m) * scale)
+                acc_s[h] = acc_s[h] * wide(alpha, 2) + jnp.dot(pr, v, preferred_element_type=F32)
+                m_s[h] = m
+
+        if late:
+            @pl.loop(0, npair)
+            def _(j):
+                full(pre_ref, j)
+
+            @pl.loop(p + 1, npair)
+            def _(j):
+                full(qkv_ref, j)
+        else:
+            @pl.loop(0, p)
+            def _(j):
+                full(qkv_ref, j)
+
+        for h in range(nh):
+            o = (acc_s[h, :, :HEAD] / acc_s[h, :, HEAD:]).astype(BF16)
+            o_s[pl.ds(2 * p, 2), :, h * HEAD:(h + 1) * HEAD] = o.reshape(2, seg, HEAD)
+
+        @pl.when(step == 0)
         def _():
-            remote(j, me).start()
-
-        @pl.when(j == me)
-        def _():
-            local().start()
-
-    @pl.when(step == npair - 1)
-    def _():
-        local().wait()
+            pl.semaphore_wait(barrier, ncp - 1)
+
+        for a in range(2):
+            j = 2 * p + a
+
+            @pl.when(j != me)
+            def _():
+                remote(j, me).start()
+
+            @pl.when(j == me)
+            def _():
+                local().start()
+
+    def cross(j, slot):
+        return pltpu.make_async_remote_copy(
+            src_ref=ex_in.at[j], dst_ref=ex_out.at[slot], send_sem=xs_sem.at[j], recv_sem=xr_sem.at[slot],
+            device_id={'cp': j}, device_id_type=pl.DeviceIdType.MESH)
+
+    def keep():
+        return pltpu.make_async_copy(ex_in.at[me], ex_out.at[me], xr_sem.at[me])
+
+    if swap:
+        for i in range(1, ncp):
+            cross(lax.rem(me + i, ncp), me).start()
+        keep().start()
+
+    local().wait()
+    for i in range(1, ncp):
+        j = lax.rem(me + i, ncp)
+        remote(j, me).wait_send()
+        remote(j, j).wait_recv()
+
+    for j in range(ncp):
+        h_s[:, j * width:(j + 1) * width] = o_r[j]
+    x_at = half * rows if x_ref.shape[0] > rows else 0
+
+    @pl.loop(0, no)
+    def _(i):
+        t = b_o + i
+        slot = ready(t)
+        cs = pl.ds(pl.multiple_of(i * TILE, TILE), TILE)
+        r = jnp.dot(h_s[...], wbuf[slot], preferred_element_type=F32)
+        xm_s[:, cs] = (x_ref[x_at:x_at + rows, cs].astype(F32) + r).astype(BF16)
+        start(t + nbuf)
+
+    _norm_to(h_s, xm_s[...], g2_ref[...])
+
+    @pl.loop(0, nf)
+    def _(i):
+        t = b_1 + 2 * i
+        s1 = ready(t)
+        s3 = ready(t + 1)
+        a = jnp.dot(h_s[...], wbuf[s1], preferred_element_type=F32)
+        b = jnp.dot(h_s[...], wbuf[s3], preferred_element_type=F32)
+        cs = pl.ds(pl.multiple_of(i * TILE, TILE), TILE)
+        u_s[:, cs] = (a * jax.nn.sigmoid(a) * b).astype(BF16)
+        start(t + nbuf)
+        start(t + 1 + nbuf)
+
+    @pl.loop(0, ny)
+    def _(i):
+        t = b_2 + kk * i
+        slots = [ready(t + k) for k in range(kk)]
+        acc = None
+        for k in range(kk):
+            r = jnp.dot(u_s[:, k * nk:(k + 1) * nk], wbuf[slots[k]], preferred_element_type=F32)
+            acc = r if acc is None else acc + r
+        cs = pl.ds(pl.multiple_of(i * TILE, TILE), TILE)
+        xm_s[:, cs] = (xm_s[:, cs].astype(F32) + acc).astype(BF16)
+        for k in range(kk):
+            start(t + k + nbuf)
+
+    y_at = half * rows if y_ref.shape[0] > rows else 0
+    y_out = pltpu.make_async_copy(xm_s, y_ref.at[pl.ds(y_at, rows)], out_sem)
+    y_out.start()
+
+    if more:
+        _norm_to(h_s, xm_s[...], g1_ref[...])
+        per = TILE // width
+
+        @pl.loop(0, nq)
+        def _(i):
+            t = b_q + 3 * i
+            slots = [ready(t + m) for m in range(3)]
+            for m in range(3):
+                r = jnp.dot(h_s[...], wbuf[slots[m]], preferred_element_type=F32)
+                for a in range(TILE // HEAD):
+                    z = r[:, a * HEAD:(a + 1) * HEAD]
+                    if m < 2:
+                        z = z * cos_ref[...] + pltpu.roll(z, HEAD // 2, 1) * sin_ref[...]
+                    lane = (a * HEAD) % width
+                    nxt_ref[i * per + (a * HEAD) // width, m, :, lane:lane + HEAD] = z.astype(BF16)
+            for m in range(3):
+                start(t + m + nbuf)
+
+    y_out.wait()
+    if swap:
+        keep().wait()
         for i in range(1, ncp):
             j = lax.rem(me + i, ncp)
-            remote(j, me).wait_send()
-            remote(j, j).wait_recv()
-
-
-def _attention(layer, late, qkv, pre):
+            cross(j, me).wait_send()
+            cross(j, j).wait_recv()
+
+
+def _layer(layer, late, x, qkv, pre, other, y, tabs, w, more):
+    g1, g2, wq, wk, wv, wo, w1, w3, w2 = w
     ncp, _, seg, width = qkv.shape
+    half = int(late)
+    d, ff = x.shape[1], w1.shape[2]
+    anyspace = pl.BlockSpec(memory_space=pl.ANY)
+    vmem = pl.BlockSpec(memory_space=pltpu.VMEM)
     nh = width // HEAD
-    npair = ncp // 2
-    whole = pl.BlockSpec((ncp, 3, seg, width), lambda p: (0, 0, 0, 0))
-    pairs = (ncp * seg) ** 2 // 2 * (3 if late else 1) * nh
+    ins, specs = [x, qkv], [vmem, vmem]
+    if late:
+        ins.append(pre)
+        specs.append(vmem)
+    ins += [g2[layer:layer + 1], wo, w1, w3, w2]
+    specs += [vmem] + [anyspace] * 4
+    outs, ospecs = [jax.ShapeDtypeStruct((seg if more else 2 * seg, d), BF16)], [anyspace]
+    block = jax.ShapeDtypeStruct(qkv.shape, BF16)
+    if more:
+        at = half * seg
+        ins += [g1[layer + 1:layer + 2], tabs[0][at:at + seg], tabs[1][at:at + seg], wq, wk, wv]
+        specs += [vmem] * 3 + [anyspace] * 3
+        outs.append(block)
+        ospecs.append(vmem)
+    if other is not None:
+        ins.append(other)
+        specs.append(anyspace)
+        outs.append(block)
+        ospecs.append(anyspace)
+    alias = {}
+    if y is not None:
+        alias = {len(ins): 0}
+        ins.append(y)
+        specs.append(anyspace)
+    dma = pltpu.SemaphoreType.DMA
+    scratch = [pltpu.VMEM((seg, d), BF16), pltpu.VMEM((RING, d, TILE), BF16), dma((RING,)),
+               pltpu.VMEM((seg, d), BF16), pltpu.VMEM((seg, ff), BF16),
+               pltpu.VMEM((ncp, seg, width), BF16), pltpu.VMEM((ncp, seg, width), BF16),
+               pltpu.VMEM((nh, 2 * seg, 2 * HEAD), F32), pltpu.VMEM((nh, 2 * seg, HEAD), F32),
+               dma((ncp,)), dma((ncp,)), dma]
+    if other is not None:
+        scratch += [dma((ncp,)), dma((ncp,))]
+    flops = 2 * seg * d * (d + 3 * ff + (3 * d if more else 0))
     return pl.pallas_call(
-        functools.partial(_attn_kernel, late),
-        grid=(npair,),
-        out_shape=jax.ShapeDtypeStruct((ncp, seg, width), BF16),
-        in_specs=[whole] * (2 if late else 1),
-        out_specs=pl.BlockSpec(memory_space=pl.ANY),
-        scratch_shapes=[pltpu.VMEM((ncp, seg, width), BF16),
-                        pltpu.VMEM((nh, 2 * seg, 2 * HEAD), F32), pltpu.VMEM((nh, 2 * seg, HEAD), F32),
-                        pltpu.SemaphoreType.DMA((ncp,)), pltpu.SemaphoreType.DMA((ncp,))],
-        compiler_params=pltpu.CompilerParams(vmem_limit_bytes=VMEM_LIMIT, dimension_semantics=("arbitrary",),
-                                             collective_id=2 * layer + int(late), has_side_effects=True),
-        cost_estimate=pl.CostEstimate(flops=pairs * HEAD * 8, bytes_accessed=8 * ncp * seg * width * 2,
-                                      transcendentals=pairs),
-        name=f"attn_{layer}_{int(late)}",
-    )(*((qkv, pre) if late else (qkv,)))
+        functools.partial(_layer_kernel, layer, late, more, other is not None, y is not None),
+        out_shape=outs,
+        in_specs=specs,
+        out_specs=ospecs,
+        scratch_shapes=scratch,
+        input_output_aliases=alias,
+        compiler_params=pltpu.CompilerParams(vmem_limit_bytes=VMEM_LIMIT, collective_id=2 * layer + half,
+                                             has_side_effects=True),
+        cost_estimate=pl.CostEstimate(flops=flops, bytes_accessed=flops // seg, transcendentals=0),
+        name=f"layer_{layer}_{half}",
+    )(*ins)
 
 
 def solution(mesh):
@@ -413,9 +589,6 @@
 
     def swap(a):
         return lax.all_to_all(a, 'cp', 0, 0, tiled=True)
-
-    def after(a, *deps):
-        return lax.optimization_barrier((a,) + deps)[0]
 
     def body(x, pos, g1, g2, wq, wk, wv, wo, w1, w3, w2):
         w = (g1, g2, wq, wk, wv, wo, w1, w3, w2)
@@ -424,18 +597,17 @@
         xs = [x, x]
         qkv = [_dense(-1, i, x, None, tabs, w, ncp, False, True)[0] for i in range(2)]
         caches = None
+        ra, other, y = swap(qkv[0]), qkv[1], None
         for l in range(layers):
             more = l + 1 < layers
-            ra = swap(qkv[0])
-            rb = swap(after(qkv[1], ra))
-            oa = _attention(l, False, ra, None)
-            res = _dense(l, 0, xs[0], oa, tabs, w, ncp, True, more)
-            ob = _attention(l, True, after(rb, res[0]), ra)
+            res = list(_layer(l, False, xs[0], ra, None, other, None, tabs, w, more))
+            xa, rb = res[0], res[-1]
+            nxt = res[1] if more else None
+            res = list(_layer(l, True, xs[1], rb, ra, nxt, None if more else xa, tabs, w, more))
             caches = _cache(l, layers, ra, rb, caches)
-            res_b = _dense(l, 1, xs[1], ob, tabs, w, ncp, True, more, None if more else res[0])
-            xs = [res[0], res_b[0]]
+            xs = [xa, res[0]]
             if more:
-                qkv = [res[1], res_b[1]]
+                other, ra = res[1], res[2]
         kc, vc = (a.reshape(layers, -1, wq.shape[2] // ncp // HEAD, HEAD) for a in caches)
         return xs[1], kc, vc
 

time: 439 us -> 353 us (0.80)
  Pallas kernels: 389 us -> 314 us
  starting transfers between devices: 20.3 us -> 6.03 us
    pallas_call x6 -> x2, Pallas kernels: 200 us -> 26.9 us  [_dense(): pl.pallas_call(functools.partial(_dense_kernel, layer, mlp, qkv, y is not...]
    pallas_call x4, Pallas kernels: 172 us -> 273 us  [_layer(): pl.pallas_call(functools.partial(_layer_kernel, layer, late, more, other...]
    all_to_all x4 -> x1, starting transfers between devices: 20.3 us -> 6.03 us  [swap(): return lax.all_to_all(a, 'cp', 0, 0, tiled=True)]
    all_to_all x4 -> x1, waiting for transfers between devices: 23.2 us -> 21 us  [swap(): return lax.all_to_all(a, 'cp', 0, 0, tiled=True)]
  transfers between devices with their start and end apart: 4 -> 1, of which waited for: 1 -> 1; matrix products, arithmetic and copies ran while one was open for 0% -> 1% of each run, Pallas kernels for 68% -> 4%
where the time goes in v3:
time: 353 us; the launch traced here: 352 us
  Pallas kernels  314 us (89%)
  waiting for transfers between devices  21 us (6%)
  starting transfers between devices  6.03 us (2%)
  local copies, waits for them, and re-layouts  5.67 us (2%)
  other arithmetic  4.87 us (1%)
    pallas_call x4, Pallas kernels, _layer(): pl.pallas_call(functools.partial(_layer_kernel, layer, late, more, other...  273 us
    pallas_call x2, Pallas kernels, _dense(): pl.pallas_call(functools.partial(_dense_kernel, layer, mlp, qkv, y is not...  26.9 us
    all_to_all x1, waiting for transfers between devices, swap(): return lax.all_to_all(a, 'cp', 0, 0, tiled=True)  21 us
    pallas_call x2, Pallas kernels, _cache(): pl.pallas_call(functools.partial(_cache_kernel, caches is None), grid=(2...  14.2 us
  transfers between devices with their start and end apart: 1, of which 1 were waited for; matrix products, arithmetic and copies ran while one was open for 1% of the time, Pallas kernels for 4%

profile of v3, /device:TPU:81, one launch (start us, length us, event | category | flops | bytes accessed | tf_op | source)
XLA Modules:
  0.0 352.3 jit_solution(5823102087105623058)
XLA Ops:
  0.6 0.7 convert_element_type.3
  1.3 1.4 fusion.6
  2.7 1.0 fusion.4
  3.7 0.0 copy-start.2
  3.7 0.0 copy-start.3
  3.7 0.7 copy-done.2
  4.4 1.0 pad_maximum_fusion
  5.4 0.0 copy-done.3
  5.4 13.5 %dense_0_0.1 = bf16[8,3,256,256]{3,2,1,0:T(8,128)(2,1)} custom-call(bf16[512,2048]{1,0:T(8,128)(2,1)} %refs_0_.7, bf16[1,2048]{1,0:T(2,128)(2,1)} %get-tuple-element.34.refs_1_, f32[512,128]{1,0:T(8,128)} %get-tuple-element.38.refs_2_, f32[512,128]{1,0:T(8,128)} %get-tuple-element.39.refs_3_, bf16[2,2048,2048]{2,1,0:T(8,128)(2,1)} %refs_11_.3, ...), custom_call_target="tpu_custom_call" | custom-call | flops 6442450944 | bytes 25165824 | tf_op jit(solution)/shard_map/dense_0_0/pallas_call | solution.py:209
  18.9 0.0 copy-start.4
  18.9 6.0 %all-to-all-start = ((bf16[8,3,256,256]{3,2,1,0:T(8,128)(2,1)}), bf16[8,3,256,256]{3,2,1,0:T(8,128)(2,1)S(1)}, u32[]{:S(2)}, u32[]{:S(2)}) async-start(bf16[8,3,256,256]{3,2,1,0:T(8,128)(2,1)} %dense_0_0.1), calls=%async_computation | async-start | bytes 6291456 | tf_op jit(solution)/shard_map/all_to_all | solution.py:591
  24.9 2.2 fusion.1
  27.1 0.0 copy-done.4
  27.1 0.6 fusion.5
  27.7 13.5 %dense_0_1.1.refs_13_ = bf16[8,3,256,256]{3,2,1,0:T(8,128)(2,1)} custom-call(bf16[512,2048]{1,0:T(8,128)(2,1)} %refs_0_.7, bf16[1,2048]{1,0:T(2,128)(2,1)} %get-tuple-element.34.refs_1_, f32[512,128]{1,0:T(8,128)} %get-tuple-element.38.refs_2_, f32[512,128]{1,0:T(8,128)} %get-tuple-element.39.refs_3_, bf16[2,2048,2048]{2,1,0:T(8,128)(2,1)} %refs_11_.3, ...), custom_call_target="tpu_custom_call" | custom-call | flops 6442450944 | bytes 25165824 | tf_op jit(solution)/shard_map/dense_0_1/pallas_call | solution.py:209
  41.2 21.0 %all-to-all-done.refs_1_.refs_2_.ka_ref.va_ref = bf16[8,3,256,256]{3,2,1,0:T(8,128)(2,1)S(1)} async-done(((bf16[8,3,256,256]{3,2,1,0:T(8,128)(2,1)}), bf16[8,3,256,256]{3,2,1,0:T(8,128)(2,1)S(1)}, u32[]{:S(2)}, u32[]{:S(2)}) %all-to-all-start) | async-done | bytes 3145760 | tf_op jit(solution)/shard_map/all_to_all | solution.py:591
  62.1 0.0 copy-start
  62.1 1.7 copy-done
  63.8 66.7 %layer_0_0.1 = (bf16[256,2048]{1,0:T(8,128)(2,1)}, bf16[8,3,256,256]{3,2,1,0:T(8,128)(2,1)}, bf16[8,3,256,256]{3,2,1,0:T(8,128)(2,1)}) custom-call(bf16[512,2048]{1,0:T(8,128)(2,1)} %refs_0_.7, bf16[8,3,256,256]{3,2,1,0:T(8,128)(2,1)} %copy-done, bf16[1,2048]{1,0:T(2,128)(2,1)} %get-tuple-element.32.refs_2_.refs_3_, bf16[2,2048,2048]{2,1,0:T(8,128)(2,1)} %refs_4_.11, ...), custom_call_target="tpu_custom_call" | custom-call | flops 34359738368 | bytes 134217728 | tf_op jit(solution)/shard_map/layer_0_0/pallas_call | solution.py:571
  130.5 72.2 %layer_0_1.1 = (bf16[256,2048]{1,0:T(8,128)(2,1)}, bf16[8,3,256,256]{3,2,1,0:T(8,128)(2,1)}, bf16[8,3,256,256]{3,2,1,0:T(8,128)(2,1)}) custom-call(bf16[512,2048]{1,0:T(8,128)(2,1)} %refs_0_.7, bf16[8,3,256,256]{3,2,1,0:T(8,128)(2,1)} %get-tuple-element.15.refs_1_.kb_ref.vb_ref, bf16[8,3,256,256]{3,2,1,0:T(8,128)(2,1)} %copy-done, ...), custom_call_target="tpu_custom_call" | custom-call | flops 34359738368 | bytes 134217728 | tf_op jit(solution)/shard_map/layer_0_1/pallas_call | solution.py:571
  202.7 59.8 %layer_1_0.1 = (bf16[512,2048]{1,0:T(8,128)(2,1)}, bf16[8,3,256,256]{3,2,1,0:T(8,128)(2,1)}) custom-call(bf16[256,2048]{1,0:T(8,128)(2,1)} %get-tuple-element.18.refs_0_, bf16[8,3,256,256]{3,2,1,0:T(8,128)(2,1)} %get-tuple-element.19.refs_1_.refs_2_.ka_ref.va_ref, bf16[1,2048]{1,0:T(2,128)(2,1)} %get-tuple-element.31.refs_2_.refs_3_, ...), custom_call_target="tpu_custom_call" | custom-call | flops 27917287424 | bytes 109051904 | tf_op jit(solution)/shard_map/layer_1_0/pallas_call | solution.py:571
  262.4 74.3 %layer_1_1.1 = bf16[512,2048]{1,0:T(8,128)(2,1)} custom-call(bf16[256,2048]{1,0:T(8,128)(2,1)} %get-tuple-element.17.refs_0_, bf16[8,3,256,256]{3,2,1,0:T(8,128)(2,1)} %get-tuple-element.21.refs_1_.kb_ref.vb_ref, bf16[8,3,256,256]{3,2,1,0:T(8,128)(2,1)} %get-tuple-element.19.refs_1_.refs_2_.ka_ref.va_ref, ...), custom_call_target="tpu_custom_call", output_to_operand_aliasing={{}: (8, {})} | custom-call | flops 27917287424 | bytes 109051904 | tf_op jit(solution)/shard_map/layer_1_1/pallas_call | solution.py:571
  336.7 7.1 %cache_0.1 = (bf16[2,8192,128]{2,1,0:T(8,128)(2,1)}, bf16[2,8192,128]{2,1,0:T(8,128)(2,1)}) custom-call(bf16[8,3,256,256]{3,2,1,0:T(8,128)(2,1)} %copy-done, bf16[8,3,256,256]{3,2,1,0:T(8,128)(2,1)} %copy-done, bf16[8,3,256,256]{3,2,1,0:T(8,128)(2,1)} %get-tuple-element.15.refs_1_.kb_ref.vb_ref, bf16[8,3,256,256]{3,2,1,0:T(8,128)(2,1)} %get-tuple-element.15.refs_1_.kb_ref.vb_ref), custom_call_target="tpu_custom_call" | custom-call | flops 4000000000 | bytes 10485760 | tf_op jit(solution)/shard_map/cache_0/pallas_call | solution.py:264
  343.8 0.0 copy-start.1
  343.8 7.2 %cache_1.1 = (bf16[2,8192,128]{2,1,0:T(8,128)(2,1)}, bf16[2,8192,128]{2,1,0:T(8,128)(2,1)}) custom-call(bf16[8,3,256,256]{3,2,1,0:T(8,128)(2,1)} %get-tuple-element.19.refs_1_.refs_2_.ka_ref.va_ref, bf16[8,3,256,256]{3,2,1,0:T(8,128)(2,1)} %get-tuple-element.19.refs_1_.refs_2_.ka_ref.va_ref, ...), custom_call_target="tpu_custom_call", output_to_operand_aliasing={{0}: (4, {}), {1}: (5, {})} | custom-call | flops 4000000000 | bytes 10485760 | tf_op jit(solution)/shard_map/cache_1/pallas_call | solution.py:264
  351.0 0.0 copy-done.1
  351.0 1.3 copy.21
  (1 shorter events, 0.0 us)
Async XLA Ops:
  3.7 0.7 copy-start.2
  3.7 1.7 copy-start.3
  18.9 8.2 %copy-start.4 = (bf16[2,2048]{1,0:T(2,128)(2,1)S(1)}, bf16[2,2048]{1,0:T(2,128)(2,1)}, u32[]{:S(2)}) copy-start(bf16[2,2048]{1,0:T(2,128)(2,1)} %param.14) | copy-start | bytes 24580
  18.9 43.3 %all-to-all-start = ((bf16[8,3,256,256]{3,2,1,0:T(8,128)(2,1)}), bf16[8,3,256,256]{3,2,1,0:T(8,128)(2,1)S(1)}, u32[]{:S(2)}, u32[]{:S(2)}) async-start(bf16[8,3,256,256]{3,2,1,0:T(8,128)(2,1)} %dense_0_0.1), calls=%async_computation | async-start | bytes 6291456 | tf_op jit(solution)/shard_map/all_to_all | solution.py:591
  62.1 1.7 copy-start
  343.8 7.2 %copy-start.1 = (bf16[512,2048]{1,0:T(8,128)(2,1)S(1)}, bf16[512,2048]{1,0:T(8,128)(2,1)}, u32[]{:S(2)}) copy-start(bf16[512,2048]{1,0:T(8,128)(2,1)} %layer_1_1.1) | copy-start | bytes 6291460

commit v4 on v3

--- a/solution.py
+++ b/solution.py
@@ -10,7 +10,7 @@
 
 HEAD = 128
 TILE = 512
-NBUF = 8
+NBUF = 9
 RING = 14
 F32 = jnp.float32
 BF16 = jnp.bfloat16
@@ -31,193 +31,115 @@
     dst[...] = (x32 * r * g.astype(F32)).astype(BF16)
 
 
-def _dense_kernel(layer, mlp, qkv, joined, *refs):
-    refs = list(refs)
-    x_ref = refs.pop(0)
-    if mlp:
-        o_ref, g2_ref, wo, w1, w3, w2 = refs[:6]
-        refs = refs[6:]
-    if qkv:
-        g1_ref, cos_ref, sin_ref, wq, wk, wv = refs[:6]
-        refs = refs[6:]
-    if joined:
-        refs.pop(0)
-    if mlp:
-        y_ref = refs.pop(0)
-    if qkv:
-        qkv_ref = refs.pop(0)
-    h_s, wbuf, sems = refs[:3]
-    if mlp:
-        xm_s, u_s = refs[3:5]
-    rows, d = x_ref.shape
-    nk = wbuf.shape[1]
-
-    segs = []
-    base = 0
-    if mlp:
-        no, nf = wo.shape[2] // TILE, w1.shape[2] // TILE
-        kk = w2.shape[1] // nk
-        ny = w2.shape[2] // TILE
-        b_o, b_1, b_2 = 0, no, no + 2 * nf
-        segs.append((b_o, no, lambda i: [(None, wo.at[layer, :, pl.ds(i * TILE, TILE)])]))
-        segs.append((b_1, 2 * nf, lambda i: [(0, w1.at[layer, :, pl.ds((i // 2) * TILE, TILE)]),
-                                             (1, w3.at[layer, :, pl.ds((i // 2) * TILE, TILE)])]))
-        segs.append((b_2, ny * kk, lambda i: [(None, w2.at[layer, pl.ds((i % kk) * nk, nk),
-                                                          pl.ds((i // kk) * TILE, TILE)])]))
-        base = b_2 + ny * kk
-    if qkv:
-        lq = layer + 1
-        nq = wq.shape[2] // TILE
-        b_q = base
-        segs.append((b_q, 3 * nq, lambda i: [(0, wq.at[lq, :, pl.ds((i // 3) * TILE, TILE)]),
-                                             (1, wk.at[lq, :, pl.ds((i // 3) * TILE, TILE)]),
-                                             (2, wv.at[lq, :, pl.ds((i // 3) * TILE, TILE)])]))
-        base = b_q + 3 * nq
-    total = base
-
-    def start(t):
-        slot = lax.rem(t, NBUF) if not isinstance(t, int) else t % NBUF
-        for b, n, srcs in segs:
-            if isinstance(t, int):
-                if b <= t < b + n:
-                    lst = srcs(t - b)
-                    src = lst[(t - b) % len(lst)][1]
-                    pltpu.make_async_copy(src, wbuf.at[slot], sems.at[slot]).start()
-                continue
-            i = t - b
-            lst = srcs(i)
-            for which, src in lst:
-                cond = (t >= b) & (t < b + n)
-                if which is not None:
-                    cond = cond & (lax.rem(i, len(lst)) == which)
-
-                @pl.when(cond)
-                def _(src=src):
-                    pltpu.make_async_copy(src, wbuf.at[slot], sems.at[slot]).start()
-
-    any_src = segs[0][2](0)[0][1]
+def _first_kernel(x_ref, g_ref, cos_ref, sin_ref, wq, wk, wv, out_ref, late_ref,
+                  h_s, wbuf, sems, qkv_s, send_sem, recv_sem):
+    me = lax.axis_index('cp')
+    ncp, _, seg, width = late_ref.shape
+    nbuf = wbuf.shape[0]
+    nq = wq.shape[2] // TILE
+    per = TILE // width
+    total = 2 * 3 * nq
+    barrier = pltpu.get_barrier_semaphore()
+    for i in range(1, ncp):
+        pl.semaphore_signal(barrier, inc=1, device_id={'cp': lax.rem(me + i, ncp)},
+                            device_id_type=pl.DeviceIdType.MESH)
+
+    def group(i):
+        return lax.rem(me // per + 1 + i, nq)
+
+    def tile(w, i):
+        return w.at[0, :, pl.ds(pl.multiple_of(group(i) * TILE, TILE), TILE)]
+
+    def start(t, which):
+        slot = t % nbuf if isinstance(t, int) else lax.rem(t, nbuf)
+        i = t // 3
+        pltpu.make_async_copy(tile((wq, wk, wv)[which], i), wbuf.at[slot], sems.at[slot]).start()
 
     def ready(t):
-        slot = lax.rem(t, NBUF)
-        pltpu.make_async_copy(any_src, wbuf.at[slot], sems.at[slot]).wait()
+        slot = lax.rem(t, nbuf)
+        pltpu.make_async_copy(tile(wq, 0), wbuf.at[slot], sems.at[slot]).wait()
         return slot
 
-    for t in range(min(NBUF, total)):
-        start(t)
-
-    if mlp:
-        for j in range(o_ref.shape[0]):
-            w = o_ref.shape[2]
-            h_s[:, j * w:(j + 1) * w] = o_ref[j]
-
-        @pl.loop(0, no)
-        def _(i):
-            t = b_o + i
-            slot = ready(t)
-            col = pl.ds(pl.multiple_of(i * TILE, TILE), TILE)
-            r = jnp.dot(h_s[...], wbuf[slot], preferred_element_type=F32)
-            xm_s[:, col] = (x_ref[:, col].astype(F32) + r).astype(BF16)
-            start(t + NBUF)
-
-        _norm_to(h_s, xm_s[...], g2_ref[...])
-
-        @pl.loop(0, nf)
-        def _(i):
-            t = b_1 + 2 * i
-            s1 = ready(t)
-            s3 = ready(t + 1)
-            a = jnp.dot(h_s[...], wbuf[s1], preferred_element_type=F32)
-            b = jnp.dot(h_s[...], wbuf[s3], preferred_element_type=F32)
-            col = pl.ds(pl.multiple_of(i * TILE, TILE), TILE)
-            u_s[:, col] = (a * jax.nn.sigmoid(a) * b).astype(BF16)
-            start(t + NBUF)
-            start(t + 1 + NBUF)
-
-        @pl.loop(0, ny)
-        def _(i):
-            t = b_2 + kk * i
-            acc = None
-            slots = [ready(t + k) for k in range(kk)]
-            for k in range(kk):
-                r = jnp.dot(u_s[:, k * nk:(k + 1) * nk], wbuf[slots[k]], preferred_element_type=F32)
-                acc = r if acc is None else acc + r
-            col = pl.ds(pl.multiple_of(i * TILE, TILE), TILE)
-            y_ref[:, col] = (xm_s[:, col].astype(F32) + acc).astype(BF16)
-            for k in range(kk):
-                start(t + k + NBUF)
-
-    if qkv:
-        _norm_to(h_s, (y_ref if mlp else x_ref)[...], g1_ref[...])
-        width = qkv_ref.shape[3]
-        per = TILE // width
+    def remote(j, slot):
+        return pltpu.make_async_remote_copy(
+            src_ref=qkv_s.at[j], dst_ref=out_ref.at[slot], send_sem=send_sem.at[j], recv_sem=recv_sem.at[slot],
+            device_id={'cp': j}, device_id_type=pl.DeviceIdType.MESH)
+
+    def local():
+        return pltpu.make_async_copy(qkv_s.at[me], out_ref.at[me], recv_sem.at[me])
+
+    for t in range(nbuf):
+        start(t, t % 3)
+
+    for half in range(2):
+        at = half * seg
+        dst = late_ref if half else qkv_s
+        _norm_to(h_s, x_ref[at:at + seg, :], g_ref[...])
 
         @pl.loop(0, nq)
         def _(i):
-            t = b_q + 3 * i
+            t = 3 * (half * nq + i)
+            gi = group(i)
             slots = [ready(t + m) for m in range(3)]
             for m in range(3):
                 r = jnp.dot(h_s[...], wbuf[slots[m]], preferred_element_type=F32)
                 for a in range(TILE // HEAD):
                     z = r[:, a * HEAD:(a + 1) * HEAD]
                     if m < 2:
-                        z = z * cos_ref[...] + pltpu.roll(z, HEAD // 2, 1) * sin_ref[...]
+                        z = (z * cos_ref[at:at + seg, :]
+                             + pltpu.roll(z, HEAD // 2, 1) * sin_ref[at:at + seg, :])
                     lane = (a * HEAD) % width
-                    qkv_ref[i * per + (a * HEAD) // width, m, :, lane:lane + HEAD] = z.astype(BF16)
-            for m in range(3):
-                start(t + m + NBUF)
-
-
-def _dense(layer, half, x, o, tabs, w, ncp, mlp, qkv, y=None):
-    g1, g2, wq, wk, wv, wo, w1, w3, w2 = w
-    rows = tabs[0].shape[0] // 2
-    d = x.shape[1]
-    ff = w1.shape[2]
+                    dst[gi * per + (a * HEAD) // width, m, :, lane:lane + HEAD] = z.astype(BF16)
+
+            @pl.when(t + 2 + nbuf < total)
+            def _():
+                for m in range(3):
+                    start(t + m + nbuf, (m + nbuf) % 3)
+
+            if half == 0:
+                @pl.when(i == 0)
+                def _():
+                    pl.semaphore_wait(barrier, ncp - 1)
+
+                for a in range(per):
+                    j = gi * per + a
+
+                    @pl.when(j != me)
+                    def _():
+                        remote(j, me).start()
+
+                    @pl.when(j == me)
+                    def _():
+                        local().start()
+
+    local().wait()
+    for i in range(1, ncp):
+        j = lax.rem(me + i, ncp)
+        remote(j, me).wait_send()
+        remote(j, j).wait_recv()
+
+
+def _first(x, tabs, w, ncp):
+    g1, _, wq, wk, wv = w[:5]
+    seg, d = x.shape[0] // 2, x.shape[1]
     width = wq.shape[2] // ncp
     anyspace = pl.BlockSpec(memory_space=pl.ANY)
     vmem = pl.BlockSpec(memory_space=pltpu.VMEM)
-
-    def part(a):
-        return pl.BlockSpec((rows, a.shape[1]), lambda i: (half if a.shape[0] > rows else 0, 0))
-
-    def whole(a):
-        return pl.BlockSpec(a.shape, lambda i: (0,) * len(a.shape))
-
-    ins, specs = [x], [part(x)]
-    outs, ospecs = [], []
-    scratch = [pltpu.VMEM((rows, d), BF16), pltpu.VMEM((NBUF, d, TILE), BF16), pltpu.SemaphoreType.DMA((NBUF,))]
-    flops = 0
-    alias = {}
-    if mlp:
-        g = g2[layer:layer + 1]
-        ins += [o, g, wo, w1, w3, w2]
-        specs += [whole(o), whole(g)] + [anyspace] * 4
-        outs.append(jax.ShapeDtypeStruct((rows if qkv else 2 * rows, d), BF16))
-        ospecs.append(part(outs[-1]))
-        scratch += [pltpu.VMEM((rows, d), BF16), pltpu.VMEM((rows, ff), BF16)]
-        flops += 2 * rows * d * (d + 3 * ff)
-    if qkv:
-        g = g1[layer + 1:layer + 2]
-        ins += [g, tabs[0], tabs[1], wq, wk, wv]
-        specs += [whole(g), part(tabs[0]), part(tabs[1])] + [anyspace] * 3
-        outs.append(jax.ShapeDtypeStruct((ncp, 3, rows, width), BF16))
-        ospecs.append(whole(outs[-1]))
-        flops += 2 * rows * d * 3 * wq.shape[2]
-    if y is not None:
-        alias = {len(ins): 0}
-        ins.append(y)
-        specs.append(anyspace)
+    block = jax.ShapeDtypeStruct((ncp, 3, seg, width), BF16)
+    dma = pltpu.SemaphoreType.DMA
+    flops = 12 * seg * d * wq.shape[2]
     return pl.pallas_call(
-        functools.partial(_dense_kernel, layer, mlp, qkv, y is not None),
-        grid=(1,),
-        out_shape=outs,
-        in_specs=specs,
-        out_specs=ospecs,
-        scratch_shapes=scratch,
-        input_output_aliases=alias,
-        compiler_params=pltpu.CompilerParams(vmem_limit_bytes=VMEM_LIMIT, dimension_semantics=("arbitrary",)),
-        cost_estimate=pl.CostEstimate(flops=flops, bytes_accessed=flops // rows, transcendentals=0),
-        name=f"dense_{layer + 1}_{half}",
-    )(*ins)
+        _first_kernel,
+        out_shape=[block, block],
+        in_specs=[vmem] * 4 + [anyspace] * 3,
+        out_specs=[anyspace, vmem],
+        scratch_shapes=[pltpu.VMEM((seg, d), BF16), pltpu.VMEM((NBUF, d, TILE), BF16), dma((NBUF,)),
+                        pltpu.VMEM(block.shape, BF16), dma((ncp,)), dma((ncp,))],
+        compiler_params=pltpu.CompilerParams(vmem_limit_bytes=VMEM_LIMIT, collective_id=2 * wq.shape[0],
+                                             has_side_effects=True),
+        cost_estimate=pl.CostEstimate(flops=flops, bytes_accessed=flops // seg, transcendentals=0),
+        name="first",
+    )(x, g1[:1], tabs[0], tabs[1], wq, wk, wv)
 
 
 def _cache_kernel(first, ka_ref, va_ref, kb_ref, vb_ref, *refs):
@@ -229,7 +151,7 @@
 
     def write(pair, order):
         for which, out in ((1, kc_ref), (2, vc_ref)):
-            for i in range(2):
+            for i in range(4):
                 src = pair[which - 1][order[i], 0]
                 for h in range(nh):
                     il_s[which - 1, pl.ds(i * seg * nh + h, seg, stride=nh), :] = (
@@ -238,22 +160,22 @@
 
     @pl.when(n < half)
     def _():
-        write((ka_ref, va_ref), (0, 1))
+        write((ka_ref, va_ref), (0, 1, 2, 3))
 
     @pl.when(n >= half)
     def _():
-        write((kb_ref, vb_ref), (1, 0))
+        write((kb_ref, vb_ref), (3, 2, 1, 0))
 
 
 def _cache(layer, layers, ra, rb, caches):
     ncp, _, seg, width = ra.shape
     nh = width // HEAD
-    npair = ncp // 2
-    rows = 2 * seg * nh
+    nq = ncp // 4
+    rows = 4 * seg * nh
     ins = [ra, ra, rb, rb]
-    block = (2, 1, seg, width)
-    specs = [pl.BlockSpec(block, lambda n, m=m: (jnp.minimum(n, npair - 1), m, 0, 0)) for m in (1, 2)]
-    specs += [pl.BlockSpec(block, lambda n, m=m: (jnp.minimum(2 * npair - 1 - n, npair - 1), m, 0, 0)) for m in (1, 2)]
+    block = (4, 1, seg, width)
+    specs = [pl.BlockSpec(block, lambda n, m=m: (jnp.minimum(n, nq - 1), m, 0, 0)) for m in (1, 2)]
+    specs += [pl.BlockSpec(block, lambda n, m=m: (jnp.minimum(2 * nq - 1 - n, nq - 1), m, 0, 0)) for m in (1, 2)]
     alias = {}
     if caches is not None:
         alias = {4: 0, 5: 1}
@@ -263,7 +185,7 @@
     spec = pl.BlockSpec((1, rows, HEAD), lambda n: (layer, n, 0))
     return pl.pallas_call(
         functools.partial(_cache_kernel, caches is None),
-        grid=(2 * npair,),
+        grid=(2 * nq,),
         out_shape=[cache, cache],
         in_specs=specs,
         out_specs=[spec, spec],
@@ -370,6 +292,18 @@
     def local():
         return pltpu.make_async_copy(o_s.at[me], o_r.at[me], recv_sem.at[me])
 
+    def cross(j, slot):
+        return pltpu.make_async_remote_copy(
+            src_ref=ex_in.at[j], dst_ref=ex_out.at[slot], send_sem=xs_sem.at[j], recv_sem=xr_sem.at[slot],
+            device_id={'cp': j}, device_id_type=pl.DeviceIdType.MESH)
+
+    def keep():
+        return pltpu.make_async_copy(ex_in.at[me], ex_out.at[me], xr_sem.at[me])
+
+    def cross_chip(k):
+        for a in range(2):
+            cross(2 * lax.rem(me // 2 + k, npair) + a, me).start()
+
     @pl.loop(0, npair)
     def _(step):
         p = lax.rem(me // 2 + 1 + step, npair)
@@ -436,17 +370,19 @@
             def _():
                 local().start()
 
-    def cross(j, slot):
-        return pltpu.make_async_remote_copy(
-            src_ref=ex_in.at[j], dst_ref=ex_out.at[slot], send_sem=xs_sem.at[j], recv_sem=xr_sem.at[slot],
-            device_id={'cp': j}, device_id_type=pl.DeviceIdType.MESH)
-
-    def keep():
-        return pltpu.make_async_copy(ex_in.at[me], ex_out.at[me], xr_sem.at[me])
+        if swap:
+            @pl.when(step == 1)
+            def _():
+                cross_chip(1)
+
+            @pl.when(step == npair - 2)
+            def _():
+                cross_chip(npair - 1)
 
     if swap:
-        for i in range(1, ncp):
-            cross(lax.rem(me + i, ncp), me).start()
+        for k in range(2, npair - 1):
+            cross_chip(k)
+        cross(me + 1 - 2 * lax.rem(me, 2), me).start()
         keep().start()
 
     local().wait()
@@ -587,17 +523,13 @@
     act = P(('req', 'cp'), None)
     cache = P(None, 'req', 'cp', None)
 
-    def swap(a):
-        return lax.all_to_all(a, 'cp', 0, 0, tiled=True)
-
     def body(x, pos, g1, g2, wq, wk, wv, wo, w1, w3, w2):
         w = (g1, g2, wq, wk, wv, wo, w1, w3, w2)
         layers = wq.shape[0]
         tabs = _tables(pos)
         xs = [x, x]
-        qkv = [_dense(-1, i, x, None, tabs, w, ncp, False, True)[0] for i in range(2)]
         caches = None
-        ra, other, y = swap(qkv[0]), qkv[1], None
+        ra, other = _first(x, tabs, w, ncp)
         for l in range(layers):
             more = l + 1 < layers
             res = list(_layer(l, False, xs[0], ra, None, other, None, tabs, w, more))

time: 353 us -> 324 us (0.918)
  waiting for transfers between devices: 21 us -> 0 us
  starting transfers between devices: 6.03 us -> 0 us
    all_to_all x1 -> x0, waiting for transfers between devices: 21 us -> none  [swap(): return lax.all_to_all(a, 'cp', 0, 0, tiled=True)]
    pallas_call x2 -> x1, Pallas kernels: 26.9 us -> 47.1 us  [_first(): pl.pallas_call(_first_kernel, out_shape=[block, block], in_specs=[vmem] *...]
    pallas_call x4, Pallas kernels: 273 us -> 259 us  [_layer(): pl.pallas_call(functools.partial(_layer_kernel, layer, late, more, other...]
    all_to_all x1 -> x0, starting transfers between devices: 6.03 us -> none  [swap(): return lax.all_to_all(a, 'cp', 0, 0, tiled=True)]
  transfers between devices with their start and end apart: 1 -> 0, of which waited for: 1 -> 0; matrix products, arithmetic and copies ran while one was open for 1% -> 0% of each run, Pallas kernels for 4% -> 0%
where the time goes in v4:
time: 324 us
  Pallas kernels  317 us (98%)
  other arithmetic  3.65 us (1%)
    pallas_call x4, Pallas kernels, _layer(): pl.pallas_call(functools.partial(_layer_kernel, layer, late, more, other...  259 us
    pallas_call x1, Pallas kernels, _first(): pl.pallas_call(_first_kernel, out_shape=[block, block], in_specs=[vmem] *...  47.1 us
    pallas_call x2, Pallas kernels, _cache(): pl.pallas_call(functools.partial(_cache_kernel, caches is None), grid=(2...  10.8 us

profile of v4, /device:TPU:81, one launch (start us, length us, event | category | flops | bytes accessed | tf_op | source)
XLA Modules:
  0.0 323.8 jit_solution(1672641956410212)
XLA Ops:
  0.6 0.7 convert_element_type.3
  1.3 1.4 fusion.5
  2.7 1.0 fusion.4
  3.7 1.0 fusion.1
  4.7 1.0 pad_maximum_fusion
  5.7 47.1 %first.1 = (bf16[8,3,256,256]{3,2,1,0:T(8,128)(2,1)}, bf16[8,3,256,256]{3,2,1,0:T(8,128)(2,1)}) custom-call(bf16[512,2048]{1,0:T(8,128)(2,1)} %refs_0_.3, bf16[1,2048]{1,0:T(2,128)(2,1)} %get-tuple-element.46.g_ref, f32[512,128]{1,0:T(8,128)} %get-tuple-element.42.cos_ref, f32[512,128]{1,0:T(8,128)} %get-tuple-element.43.sin_ref, ...), custom_call_target="tpu_custom_call" | custom-call | flops 12884901888 | bytes 50331648 | tf_op jit(solution)/shard_map/first/pallas_call | solution.py:131
  52.8 67.2 %layer_0_0.1 = (bf16[256,2048]{1,0:T(8,128)(2,1)}, bf16[8,3,256,256]{3,2,1,0:T(8,128)(2,1)}, bf16[8,3,256,256]{3,2,1,0:T(8,128)(2,1)}) custom-call(bf16[512,2048]{1,0:T(8,128)(2,1)} %refs_0_.3, bf16[8,3,256,256]{3,2,1,0:T(8,128)(2,1)} %get-tuple-element.17.refs_1_.refs_2_.ka_ref.va_ref, bf16[1,2048]{1,0:T(2,128)(2,1)} %get-tuple-element.36.refs_2_.refs_3_, ...), custom_call_target="tpu_custom_call" | custom-call | flops 34359738368 | bytes 134217728 | tf_op jit(solution)/shard_map/layer_0_0/pallas_call | solution.py:507
  120.0 72.2 %layer_0_1.1 = (bf16[256,2048]{1,0:T(8,128)(2,1)}, bf16[8,3,256,256]{3,2,1,0:T(8,128)(2,1)}, bf16[8,3,256,256]{3,2,1,0:T(8,128)(2,1)}) custom-call(bf16[512,2048]{1,0:T(8,128)(2,1)} %refs_0_.3, bf16[8,3,256,256]{3,2,1,0:T(8,128)(2,1)} %get-tuple-element.19.refs_1_.kb_ref.vb_ref, bf16[8,3,256,256]{3,2,1,0:T(8,128)(2,1)} %get-tuple-element.17.refs_1_.refs_2_.ka_ref.va_ref, ...), custom_call_target="tpu_custom_call" | custom-call | flops 34359738368 | bytes 134217728 | tf_op jit(solution)/shard_map/layer_0_1/pallas_call | solution.py:507
  192.2 5.3 %cache_0.1 = (bf16[2,8192,128]{2,1,0:T(8,128)(2,1)}, bf16[2,8192,128]{2,1,0:T(8,128)(2,1)}) custom-call(bf16[8,3,256,256]{3,2,1,0:T(8,128)(2,1)} %get-tuple-element.17.refs_1_.refs_2_.ka_ref.va_ref, bf16[8,3,256,256]{3,2,1,0:T(8,128)(2,1)} %get-tuple-element.17.refs_1_.refs_2_.ka_ref.va_ref, ...), custom_call_target="tpu_custom_call" | custom-call | flops 4000000000 | bytes 10485760 | tf_op jit(solution)/shard_map/cache_0/pallas_call | solution.py:186
  197.5 56.5 %layer_1_0.1 = (bf16[512,2048]{1,0:T(8,128)(2,1)}, bf16[8,3,256,256]{3,2,1,0:T(8,128)(2,1)}) custom-call(bf16[256,2048]{1,0:T(8,128)(2,1)} %get-tuple-element.22.refs_0_, bf16[8,3,256,256]{3,2,1,0:T(8,128)(2,1)} %get-tuple-element.23.refs_1_.refs_2_.ka_ref.va_ref, bf16[1,2048]{1,0:T(2,128)(2,1)} %get-tuple-element.35.refs_2_.refs_3_, ...), custom_call_target="tpu_custom_call" | custom-call | flops 27917287424 | bytes 109051904 | tf_op jit(solution)/shard_map/layer_1_0/pallas_call | solution.py:507
  254.0 63.0 %layer_1_1.1 = bf16[512,2048]{1,0:T(8,128)(2,1)} custom-call(bf16[256,2048]{1,0:T(8,128)(2,1)} %get-tuple-element.21.refs_0_, bf16[8,3,256,256]{3,2,1,0:T(8,128)(2,1)} %get-tuple-element.25.refs_1_.kb_ref.vb_ref, bf16[8,3,256,256]{3,2,1,0:T(8,128)(2,1)} %get-tuple-element.23.refs_1_.refs_2_.ka_ref.va_ref, ...), custom_call_target="tpu_custom_call", output_to_operand_aliasing={{}: (8, {})} | custom-call | flops 27917287424 | bytes 109051904 | tf_op jit(solution)/shard_map/layer_1_1/pallas_call | solution.py:507
  317.0 0.0 copy-start
  317.0 5.5 %cache_1.1 = (bf16[2,8192,128]{2,1,0:T(8,128)(2,1)}, bf16[2,8192,128]{2,1,0:T(8,128)(2,1)}) custom-call(bf16[8,3,256,256]{3,2,1,0:T(8,128)(2,1)} %get-tuple-element.23.refs_1_.refs_2_.ka_ref.va_ref, bf16[8,3,256,256]{3,2,1,0:T(8,128)(2,1)} %get-tuple-element.23.refs_1_.refs_2_.ka_ref.va_ref, ...), custom_call_target="tpu_custom_call", output_to_operand_aliasing={{0}: (4, {}), {1}: (5, {})} | custom-call | flops 4000000000 | bytes 10485760 | tf_op jit(solution)/shard_map/cache_1/pallas_call | solution.py:186
  322.5 0.0 copy-done
  322.5 1.3 copy.21
  (1 shorter events, 0.0 us)
Async XLA Ops:
  317.0 5.5 %copy-start = (bf16[512,2048]{1,0:T(8,128)(2,1)S(1)}, bf16[512,2048]{1,0:T(8,128)(2,1)}, u32[]{:S(2)}) copy-start(bf16[512,2048]{1,0:T(8,128)(2,1)} %layer_1_1.1) | copy-start | bytes 6291460
